TPU v7x, 32 devices: a whole 2x2x4 slice. The times are simulated.
32 devices in a mesh: slab: 8 (over y, x, core), det: 4 (over z).
Axes of the slice: x: 2, y: 2, z: 4, core: 2. Of those that a mesh axis runs over, the one named last changes fastest.
Arguments:
- traces: float32 [32, 128, 4096], P(('slab', 'det')), may hold values from -6 to 6
- tables: bfloat16 [32, 256, 2048], P('slab', None, 'det'), may hold values from -0.0625 to 0.0625
- slab_range: int32 [32, 2], P(('slab', 'det')), may hold values from 0 to 7, as said below
- table_slot: int32 [32, 7], P(('slab', 'det')), may hold values from 0 to 3
- sample_start: int32 [32, 7], P(('slab', 'det')), may hold values from 0 to 3840
Outputs:
- image: float32 [128, 16384], P(None, ('slab', 'det'))
Inputs may be any that keep to these rules, and one draw needn't show every extreme that they name: For detector d with home slab g = d // 4: max(0, g - 3) <= slab_range[d, 0] <= g <= slab_range[d, 1] <= min(7, g + 3); some detectors reach the full 3 on both sides where the grid allows.
All inputs are finite; a program needn't handle non-finite values.
Results may differ from a plain program's by a relative error of at most 0.007.
Values may be sent and summed in bfloat16 or wider, within the bound.
A program may use at most 64 MiB of HBM per device.

v0:
```python
import functools

import jax
import jax.numpy as jnp
from jax import lax
from jax.experimental import pallas as pl
from jax.experimental.pallas import tpu as pltpu
from jax.sharding import PartitionSpec as P

MESH = pl.DeviceIdType.MESH
KWIN = 256
NTAB = 4
RANGE = 3
LANES = 128
OFFSETS = 2 * RANGE + 1
CUT_LIMIT = 16 * 1024 * 1024


def cut_kernel(n_slab, traces, whole, wins, masks, spans, sems):
    slab = lax.axis_index("slab")
    samp, span = traces.shape[2], spans.shape[2]
    n_quarter, _, rows, _ = wins.shape
    loads, inner = [], []
    for o in range(OFFSETS):
        start = whole[0, 2 + OFFSETS + o]
        tile = jnp.minimum(lax.div(start, LANES), (samp - span) // LANES)
        inner.append(start - tile * LANES)
        first = pl.multiple_of(tile * LANES, LANES)
        loads.append(
            pltpu.make_async_copy(traces.at[0, :, pl.ds(first, span)], spans.at[o], sems.at[o])
        )
        loads[-1].start()
    mask_rows = lax.broadcasted_iota(jnp.int32, masks.shape[1:], 0)
    for o in range(OFFSETS):
        target = slab + (o - RANGE)
        active = (whole[0, 0] <= target) & (target <= whole[0, 1])
        slot = jnp.where(active, whole[0, 2 + o], -1)
        masks[o] = (mask_rows == slot).astype(jnp.float32)
    far = lax.broadcasted_iota(jnp.int32, (span, KWIN), 0)
    far = far - lax.broadcasted_iota(jnp.int32, (span, KWIN), 1)
    for o in range(OFFSETS):
        pick = (far == inner[o]).astype(jnp.bfloat16)
        loads[o].wait()
        moved = jnp.dot(spans[o].astype(jnp.bfloat16), pick, preferred_element_type=jnp.float32)
        for q in range(n_quarter):
            wins[q, o] = moved[q * rows : (q + 1) * rows].astype(jnp.bfloat16)


def kernel(
    n_slab, n_det,
    send_win, send_mask, tables, out,
    table_buf, got_win, got_mask,
    part, got_part, total, got_total,
    table_sem, win_send, win_recv, mask_send, mask_recv,
    part_send, part_recv, total_send, total_recv,
):
    slab, det = lax.axis_index("slab"), lax.axis_index("det")
    rows = send_win.shape[2]
    order = sorted(range(1, n_det), key=lambda d: -min(d, n_det - d)) + [0]
    away = [o for o in range(OFFSETS) if o != RANGE]
    away.sort(key=lambda o: -abs(o - RANGE))

    def valid(to):
        return (to >= 0) & (to < n_slab)

    def part_of(d):
        return lax.rem(det + d, n_det)

    table_load = pltpu.make_async_copy(tables, table_buf, table_sem)
    table_load.start()

    barrier = pltpu.get_barrier_semaphore()
    peers = jnp.int32(n_det - 1)
    for o in away:
        peer = slab + (o - RANGE)
        peers = peers + valid(peer).astype(jnp.int32)

        @pl.when(valid(peer))
        def _():
            pl.semaphore_signal(barrier, 1, device_id=(peer, det), device_id_type=MESH)

    for d in order[:-1]:
        pl.semaphore_signal(
            barrier, 1, device_id=(slab, part_of(d)), device_id_type=MESH
        )

    def mask_copy(o):
        return pltpu.make_async_remote_copy(
            src_ref=send_mask.at[o], dst_ref=got_mask.at[o],
            send_sem=mask_send.at[o], recv_sem=mask_recv.at[o],
            device_id=(slab + (o - RANGE), det), device_id_type=MESH,
        )

    def win_copy(c, o):
        return pltpu.make_async_remote_copy(
            src_ref=send_win.at[part_of(order[c]), o], dst_ref=got_win.at[c, o],
            send_sem=win_send.at[c, o], recv_sem=win_recv.at[c, o],
            device_id=(slab + (o - RANGE), det), device_id_type=MESH,
        )

    def part_copy(c):
        d = order[c]
        return pltpu.make_async_remote_copy(
            src_ref=part.at[c], dst_ref=got_part.at[c],
            send_sem=part_send.at[c], recv_sem=part_recv.at[c],
            device_id=(slab, part_of(d)), device_id_type=MESH,
        )

    def total_copy(c):
        d = order[c]
        return pltpu.make_async_remote_copy(
            src_ref=total, dst_ref=got_total.at[c],
            send_sem=total_send.at[c], recv_sem=total_recv.at[c],
            device_id=(slab, part_of(d)), device_id_type=MESH,
        )

    pl.semaphore_wait(barrier, peers)
    for c in range(n_det):
        for o in away:

            @pl.when(valid(slab + (o - RANGE)))
            def _():
                if c == 0:
                    mask_copy(o).start()
                win_copy(c, o).start()

    for o in away:

        @pl.when(jnp.logical_not(valid(slab - (o - RANGE))))
        def _():
            got_mask[o] = jnp.zeros(got_mask.shape[1:], got_mask.dtype)
            for c in range(n_det):
                got_win[c, o] = jnp.zeros(got_win.shape[2:], got_win.dtype)

    for c in range(n_det):
        for o in away:

            @pl.when(valid(slab - (o - RANGE)))
            def _():
                if c == 0:
                    mask_copy(o).wait_recv()
                win_copy(c, o).wait_recv()

        bins = [jnp.zeros((rows, KWIN), jnp.float32) for _ in range(NTAB)]
        for o in range(OFFSETS):
            if o == RANGE:
                win, mask = send_win[part_of(order[c]), o], send_mask
            else:
                win, mask = got_win[c, o], got_mask
            win = win.astype(jnp.float32)
            for t in range(NTAB):
                weight = jnp.concatenate([mask[o, t : t + 1]] * (KWIN // LANES), axis=1)
                bins[t] = bins[t] + weight * win
        for t in range(NTAB):
            part[c, :, t * KWIN : (t + 1) * KWIN] = bins[t].astype(jnp.bfloat16)
        if order[c] != 0:
            part_copy(c).start()

    summed = part[n_det - 1].astype(jnp.float32)
    for c in range(n_det - 1):
        part_copy(c).wait_recv()
        summed = summed + got_part[c].astype(jnp.float32)
    total[...] = summed.astype(jnp.bfloat16)
    for c in range(n_det - 1):
        total_copy(c).start()

    table_load.wait()
    weights = table_buf[...].reshape(NTAB * KWIN, table_buf.shape[2])

    def finish(quarter_sum, d):
        out[pl.ds(pl.multiple_of(part_of(d) * rows, rows), rows), :] = jnp.dot(
            quarter_sum, weights, preferred_element_type=jnp.float32
        )

    finish(total[...], 0)
    nearest = sorted(range(n_det - 1), key=lambda c: min(order[c], n_det - order[c]))
    for c in nearest:
        total_copy(c).wait_recv()
        finish(got_total[c], n_det - order[c])

    for o in away:

        @pl.when(valid(slab + (o - RANGE)))
        def _():
            mask_copy(o).wait_send()
            for c in range(n_det):
                win_copy(c, o).wait_send()

    for c in range(n_det - 1):
        part_copy(c).wait_send()
        total_copy(c).wait_send()


def body(n_slab, n_det, traces, tables, slab_range, table_slot, sample_start):
    _, frames, samp = traces.shape
    voxels = tables.shape[2]
    rows = frames // n_det
    wide = NTAB * KWIN
    mask_rows = -(-NTAB // 8) * 8
    anywhere = pl.BlockSpec(memory_space=pl.ANY)
    scalars = pl.BlockSpec(memory_space=pltpu.SMEM)
    vmem = pl.BlockSpec(memory_space=pltpu.VMEM)
    dma = pltpu.SemaphoreType.DMA
    wins, masks = pl.pallas_call(
        functools.partial(cut_kernel, n_slab),
        out_shape=[
            jax.ShapeDtypeStruct((n_det, OFFSETS, rows, KWIN), jnp.bfloat16),
            jax.ShapeDtypeStruct((OFFSETS, mask_rows, LANES), jnp.float32),
        ],
        in_specs=[pl.BlockSpec(memory_space=pltpu.HBM), scalars],
        out_specs=[vmem, vmem],
        scratch_shapes=[
            pltpu.VMEM((OFFSETS, frames, KWIN + LANES), jnp.float32),
            dma((OFFSETS,)),
        ],
        compiler_params=pltpu.CompilerParams(vmem_limit_bytes=CUT_LIMIT),
    )(traces, jnp.concatenate([slab_range, table_slot, sample_start], axis=1))
    return pl.pallas_call(
        functools.partial(kernel, n_slab, n_det),
        out_shape=jax.ShapeDtypeStruct((frames, voxels), jnp.float32),
        in_specs=[vmem, vmem, anywhere],
        out_specs=vmem,
        scratch_shapes=[
            pltpu.VMEM(tables.shape, jnp.bfloat16),
            pltpu.VMEM((n_det, OFFSETS, rows, KWIN), jnp.bfloat16),
            pltpu.VMEM((OFFSETS, mask_rows, LANES), jnp.float32),
            pltpu.VMEM((n_det, rows, wide), jnp.bfloat16),
            pltpu.VMEM((n_det, rows, wide), jnp.bfloat16),
            pltpu.VMEM((rows, wide), jnp.bfloat16),
            pltpu.VMEM((n_det, rows, wide), jnp.bfloat16),
            dma,
            dma((n_det, OFFSETS)),
            dma((n_det, OFFSETS)),
            dma((OFFSETS,)),
            dma((OFFSETS,)),
            dma((n_det,)),
            dma((n_det,)),
            dma((n_det,)),
            dma((n_det,)),
        ],
        compiler_params=pltpu.CompilerParams(
            collective_id=0, has_side_effects=True, vmem_limit_bytes=16 * 1024 * 1024
        ),
    )(wins, masks, tables)


def solution(mesh):
    placed = (
        P(("slab", "det"), None, None),
        P("slab", None, "det"),
        P(("slab", "det"), None),
        P(("slab", "det"), None),
        P(("slab", "det"), None),
    )
    return jax.shard_map(
        functools.partial(body, mesh.shape["slab"], mesh.shape["det"]),
        mesh=mesh, in_specs=placed, out_specs=P(None, ("slab", "det")), check_vma=False,
    )
```

profile of v0, /device:TPU:0, one launch (start us, length us, event | category | flops | bytes accessed | tf_op | source)
XLA Modules:
  0.0 30.7 jit_solution(18162639300528524921)
XLA Ops:
  0.0 0.8 %pad_add_fusion.whole = s32[1,16]{1,0:T(1,128)S(1)} fusion(s32[1,7]{1,0:T(1,128)} %param.9, s32[1,7]{1,0:T(1,128)} %param.8, s32[1,2]{1,0:T(1,128)} %param.7), kind=kLoop, calls=%fused_computation | loop fusion | flops 32 | bytes 128 | tf_op jit(solution)/shard_map/concatenate | solution.py:217
  0.8 0.0 copy-start
  0.8 1.6 %copy-done = f32[1,128,4096]{2,1,0:T(8,128)S(1)} copy-done((f32[1,128,4096]{2,1,0:T(8,128)S(1)}, f32[1,128,4096]{2,1,0:T(8,128)}, u32[]{:S(2)}) %copy-start) | copy-done | bytes 2097176
  2.4 0.0 copy-start.1
  2.4 2.3 %shard_map.55 = (bf16[4,7,32,256]{3,2,1,0:T(8,128)(2,1)S(1)}, f32[7,8,128]{2,1,0:T(8,128)S(1)}) custom-call(f32[1,128,4096]{2,1,0:T(8,128)S(1)} %copy-done, s32[1,16]{1,0:T(1,128)S(1)} %pad_add_fusion.whole), custom_call_target="tpu_custom_call" | custom-call | tf_op jit(solution)/shard_map/pallas_call | solution.py:204
  4.7 0.0 copy-done.1
  4.7 25.2 %shard_map.56 = f32[128,512]{1,0:T(8,128)S(1)} custom-call(bf16[4,7,32,256]{3,2,1,0:T(8,128)(2,1)S(1)} %get-tuple-element.7.send_win, f32[7,8,128]{2,1,0:T(8,128)S(1)} %get-tuple-element.8.send_mask, bf16[4,256,512]{2,1,0:T(8,128)(2,1)S(1)} %copy-done.1), custom_call_target="tpu_custom_call" | custom-call | tf_op jit(solution)/shard_map/pallas_call | solution.py:218
  29.9 0.7 %copy.7 = f32[128,512]{1,0:T(8,128)} copy(f32[128,512]{1,0:T(8,128)S(1)} %shard_map.56) | data formatting | bytes 524288
Async XLA Ops:
  0.8 1.6 %copy-start = (f32[1,128,4096]{2,1,0:T(8,128)S(1)}, f32[1,128,4096]{2,1,0:T(8,128)}, u32[]{:S(2)}) copy-start(f32[1,128,4096]{2,1,0:T(8,128)} %traces.1) | copy-start | bytes 6291460
  2.4 2.3 %copy-start.1 = (bf16[4,256,512]{2,1,0:T(8,128)(2,1)S(1)}, bf16[4,256,512]{2,1,0:T(8,128)(2,1)}, u32[]{:S(2)}) copy-start(bf16[4,256,512]{2,1,0:T(8,128)(2,1)} %tables.1) | copy-start | bytes 3145732
where the time goes:
time: 30.8 us; the launch traced here: 30.7 us
  Pallas kernels  27.6 us (90%)
  local copies, waits for them, and re-layouts  2.3 us (7%)
  other arithmetic  0.76 us (2%)
    pallas_call x1, Pallas kernels, body(): pl.pallas_call(functools.partial(kernel, n_slab, n_det), out_shape=jax.Sh...  25.2 us
    pallas_call x1, Pallas kernels, body(): pl.pallas_call(functools.partial(cut_kernel, n_slab), out_shape=[jax.Shap...  2.32 us
    unnamed x5, local copies, waits for them, and re-layouts  2.3 us
    concatenate x1, other arithmetic, body(): jnp.concatenate([slab_range, table_slot, sample_start], axis=1)  0.76 us

commit v1 on v0

v1 whole, which is shorter than its diff:
```python
import functools

import jax
import jax.numpy as jnp
from jax import lax
from jax.experimental import pallas as pl
from jax.experimental.pallas import tpu as pltpu
from jax.sharding import PartitionSpec as P

MESH = pl.DeviceIdType.MESH
KWIN = 256
NTAB = 4
RANGE = 3
LANES = 128
OFFSETS = 2 * RANGE + 1
ROWS = 16
LAG = 4
WORK = jnp.float32
BITS = (1, 2, 4, 8, 16, 32, 64)
AWAY = [o for o in range(OFFSETS) if o != RANGE]


def kernel(
    n_slab, n_det,
    traces, tables, slab_range, table_slot, sample_start, out,
    table_buf, range_buf, slot_buf, start_buf,
    send_win, got_win, send_mask, got_mask,
    own, up, from_outer, from_inner, down,
    trace_sem, table_sem, small_sem,
    win_send, win_recv, mask_send, mask_recv,
    up_send, outer_recv, down_send, inner_recv,
    *trace_bufs,
):
    slab, det = lax.axis_index("slab"), lax.axis_index("det")
    n_chunk = send_win.shape[0]
    half = n_det // 2

    smalls = [
        pltpu.make_async_copy(src, dst, small_sem.at[i])
        for i, (src, dst) in enumerate(
            [(sample_start, start_buf), (slab_range, range_buf), (table_slot, slot_buf)]
        )
    ]
    for copy in smalls:
        copy.start()

    def rows_of(c):
        return pl.ds(c * ROWS, ROWS)

    loads = [
        pltpu.make_async_copy(traces.at[0, rows_of(c)], trace_bufs[c], trace_sem.at[c])
        for c in range(n_chunk)
    ]
    for copy in loads:
        copy.start()
    table_load = pltpu.make_async_copy(tables, table_buf, table_sem)
    table_load.start()

    def valid(to):
        return (to >= 0) & (to < n_slab)

    left = det < half
    inner = jnp.where(left, det + 1, det - 1)
    outer = jnp.where(left, det - 1, det + 1)

    barrier = pltpu.get_barrier_semaphore()
    peers = jnp.int32(0)
    for o in AWAY:
        peer = slab + (o - RANGE)
        peers = peers + valid(peer).astype(jnp.int32)

        @pl.when(valid(peer))
        def _():
            pl.semaphore_signal(barrier, 1, device_id=(peer, det), device_id_type=MESH)

    for step in (-1, 1):
        near = det + step
        there = (near >= 0) & (near < n_det)
        peers = peers + there.astype(jnp.int32)

        @pl.when(there)
        def _():
            pl.semaphore_signal(barrier, 1, device_id=(slab, near), device_id_type=MESH)

    for o in AWAY:

        @pl.when(jnp.logical_not(valid(slab - (o - RANGE))))
        def _():
            got_mask[o] = jnp.zeros(got_mask.shape[1:], got_mask.dtype)
            for c in range(n_chunk):
                got_win[c, o] = jnp.zeros(got_win.shape[2:], got_win.dtype)

    def mask_copy(o):
        return pltpu.make_async_remote_copy(
            src_ref=send_mask.at[o], dst_ref=got_mask.at[o],
            send_sem=mask_send.at[o], recv_sem=mask_recv.at[o],
            device_id=(slab + (o - RANGE), det), device_id_type=MESH,
        )

    def win_copy(c, o):
        return pltpu.make_async_remote_copy(
            src_ref=send_win.at[c, o], dst_ref=got_win.at[c, o],
            send_sem=win_send.at[c, o], recv_sem=win_recv.at[c, o],
            device_id=(slab + (o - RANGE), det), device_id_type=MESH,
        )

    def up_copy(c, cross):
        return pltpu.make_async_remote_copy(
            src_ref=up.at[c], dst_ref=(from_inner if cross else from_outer).at[c],
            send_sem=up_send.at[c], recv_sem=(inner_recv if cross else outer_recv).at[c],
            device_id=(slab, inner), device_id_type=MESH,
        )

    def down_copy(c):
        return pltpu.make_async_remote_copy(
            src_ref=down.at[c], dst_ref=from_inner.at[c],
            send_sem=down_send.at[c], recv_sem=inner_recv.at[c],
            device_id=(slab, outer), device_id_type=MESH,
        )

    for copy in smalls:
        copy.wait()
    n_tile = traces.shape[2] // LANES
    steps = [1 << b for b in reversed(range((n_tile - 1).bit_length()))]
    lane = lax.broadcasted_iota(jnp.int32, (ROWS, LANES), 1)
    mask_rows = lax.broadcasted_iota(jnp.int32, send_mask.shape[1:], 0)
    hits, turns, keeps = [], [], []
    for o in range(OFFSETS):
        target = slab + (o - RANGE)
        low, high, slot = (
            jnp.full(mask_rows.shape, value)
            for value in (range_buf[0, 0], range_buf[0, 1], slot_buf[0, o])
        )
        hit = (low <= target) & (target <= high) & (mask_rows == slot)
        send_mask[o] = hit.astype(jnp.float32)
        start = jnp.full(lane.shape, start_buf[0, o])
        hits.append([(start & (step * LANES)) != 0 for step in steps])
        turns.append([(start & bit) != 0 for bit in BITS])
        keeps.append(lane < LANES - (start & (LANES - 1)))

    def window(c, o):
        def tile(i):
            i = min(i, n_tile - 1)
            return trace_bufs[c][:, i * LANES : (i + 1) * LANES].astype(WORK)

        tiles = None
        for step, hit in zip(steps, hits[o]):
            get = tile if tiles is None else tiles.__getitem__
            tiles = [jnp.where(hit, get(i + step), get(i)) for i in range(step + 2)]
        for bit, hit in zip(BITS, turns[o]):
            tiles = [jnp.where(hit, pltpu.roll(x, LANES - bit, 1), x) for x in tiles]
        for i in range(KWIN // LANES):
            piece = jnp.where(keeps[o], tiles[i], tiles[i + 1])
            send_win[c, o, :, i * LANES : (i + 1) * LANES] = piece.astype(jnp.bfloat16)

    for c in range(n_chunk):
        loads[c].wait()
        for o in range(OFFSETS):
            window(c, o)
        if c == 0:
            pl.semaphore_wait(barrier, peers)
        for o in AWAY:

            @pl.when(valid(slab + (o - RANGE)))
            def _():
                if c == 0:
                    mask_copy(o).start()
                win_copy(c, o).start()

    def stack(c):
        for o in AWAY:

            @pl.when(valid(slab - (o - RANGE)))
            def _():
                if c == 0:
                    mask_copy(o).wait_recv()
                win_copy(c, o).wait_recv()

        bins = [jnp.zeros((ROWS, KWIN), jnp.float32) for _ in range(NTAB)]
        for o in range(OFFSETS):
            if o == RANGE:
                win, mask = send_win[c, o], send_mask
            else:
                win, mask = got_win[c, o], got_mask
            win = win.astype(jnp.float32)
            for t in range(NTAB):
                weight = jnp.concatenate([mask[o, t : t + 1]] * (KWIN // LANES), axis=1)
                bins[t] = bins[t] + weight * win
        return bins

    def cols(t):
        return slice(t * KWIN, (t + 1) * KWIN)

    def weights():
        return table_buf[...].reshape(NTAB * KWIN, table_buf.shape[2])

    def image(ref, c, n):
        sums = ref[c : c + n].reshape(n * ROWS, NTAB * KWIN)
        out[c * ROWS : (c + n) * ROWS] = jnp.dot(
            sums, weights(), preferred_element_type=jnp.float32
        )

    def role(has_outer, cross):
        def send_up(c):
            bins = stack(c)
            if has_outer:
                up_copy(c, False).wait_recv()
            for t in range(NTAB):
                total = bins[t]
                if has_outer:
                    total = total + from_outer[c, :, cols(t)].astype(jnp.float32)
                if cross:
                    own[c, :, cols(t)] = total
                up[c, :, cols(t)] = total.astype(jnp.bfloat16)
            up_copy(c, cross).start()

        def send_down(c):
            down_copy(c).wait_recv()
            if cross:
                for t in range(NTAB):
                    total = own[c, :, cols(t)] + from_inner[c, :, cols(t)].astype(jnp.float32)
                    down[c, :, cols(t)] = total.astype(jnp.bfloat16)
            else:
                down[c] = from_inner[c]
            down_copy(c).start()

        if has_outer or cross:
            for i in range(n_chunk + LAG):
                if i < n_chunk:
                    send_up(i)
                if i >= LAG:
                    send_down(i - LAG)
            table_load.wait()
            image(down, 0, n_chunk)
        else:
            for c in range(n_chunk):
                send_up(c)
            table_load.wait()
            pair = 2
            for c in range(n_chunk):
                down_copy(c).wait_recv()
                if c % pair == pair - 1:
                    image(from_inner, c + 1 - pair, pair)
        for c in range(n_chunk):
            up_copy(c, cross).wait_send()
            if has_outer:
                down_copy(c).wait_send()

    edge = (det == 0) | (det == n_det - 1)
    pl.when(edge)(lambda: role(False, False))
    pl.when(jnp.logical_not(edge))(lambda: role(True, True))

    for o in AWAY:

        @pl.when(valid(slab + (o - RANGE)))
        def _():
            mask_copy(o).wait_send()
            for c in range(n_chunk):
                win_copy(c, o).wait_send()


def body(n_slab, n_det, traces, tables, slab_range, table_slot, sample_start):
    _, frames, samp = traces.shape
    voxels = tables.shape[2]
    n_chunk = frames // ROWS
    wide = NTAB * KWIN
    mask_rows = -(-NTAB // 8) * 8
    anywhere = pl.BlockSpec(memory_space=pl.ANY)
    dma = pltpu.SemaphoreType.DMA
    return pl.pallas_call(
        functools.partial(kernel, n_slab, n_det),
        out_shape=pltpu.VMEM((frames, voxels), jnp.float32),
        in_specs=[anywhere] * 5,
        out_specs=pl.BlockSpec(memory_space=pltpu.VMEM),
        scratch_shapes=[
            pltpu.VMEM(tables.shape, jnp.bfloat16),
            pltpu.SMEM(slab_range.shape, jnp.int32),
            pltpu.SMEM(table_slot.shape, jnp.int32),
            pltpu.SMEM(sample_start.shape, jnp.int32),
            pltpu.VMEM((n_chunk, OFFSETS, ROWS, KWIN), jnp.bfloat16),
            pltpu.VMEM((n_chunk, OFFSETS, ROWS, KWIN), jnp.bfloat16),
            pltpu.VMEM((OFFSETS, mask_rows, LANES), jnp.float32),
            pltpu.VMEM((OFFSETS, mask_rows, LANES), jnp.float32),
            pltpu.VMEM((n_chunk, ROWS, wide), jnp.float32),
            pltpu.VMEM((n_chunk, ROWS, wide), jnp.bfloat16),
            pltpu.VMEM((n_chunk, ROWS, wide), jnp.bfloat16),
            pltpu.VMEM((n_chunk, ROWS, wide), jnp.bfloat16),
            pltpu.VMEM((n_chunk, ROWS, wide), jnp.bfloat16),
            dma((n_chunk,)),
            dma,
            dma((3,)),
            dma((n_chunk, OFFSETS)),
            dma((n_chunk, OFFSETS)),
            dma((OFFSETS,)),
            dma((OFFSETS,)),
            dma((n_chunk,)),
            dma((n_chunk,)),
            dma((n_chunk,)),
            dma((n_chunk,)),
            *[pltpu.VMEM((ROWS, samp), jnp.float32) for _ in range(n_chunk)],
        ],
        compiler_params=pltpu.CompilerParams(
            collective_id=0, has_side_effects=True, vmem_limit_bytes=66_500_000
        ),
    )(traces, tables, slab_range, table_slot, sample_start)


def solution(mesh):
    placed = (
        P(("slab", "det"), None, None),
        P("slab", None, "det"),
        P(("slab", "det"), None),
        P(("slab", "det"), None),
        P(("slab", "det"), None),
    )
    return jax.shard_map(
        functools.partial(body, mesh.shape["slab"], mesh.shape["det"]),
        mesh=mesh, in_specs=placed, out_specs=P(None, ("slab", "det")), check_vma=False,
    )
```

time: 30.8 us -> 25.2 us (0.82)
  Pallas kernels: 27.6 us -> 24.3 us
  local copies, waits for them, and re-layouts: 2.3 us -> 0.71 us
  other arithmetic: 0.76 us -> 0 us
    pallas_call x2 -> x1, Pallas kernels: 27.6 us -> 24.3 us  [body(): pl.pallas_call(functools.partial(kernel, n_slab, n_det), out_shape=pltpu....]
    unnamed x5 -> x1, local copies, waits for them, and re-layouts: 2.3 us -> 0.71 us
    concatenate x1 -> x0, other arithmetic: 0.76 us -> none  [body(): jnp.concatenate([slab_range, table_slot, sample_start], axis=1)]
where the time goes in v1:
time: 25.2 us; the launch traced here: 25.1 us
  Pallas kernels  24.3 us (96%)
  local copies, waits for them, and re-layouts  0.71 us (3%)
    pallas_call x1, Pallas kernels, body(): pl.pallas_call(functools.partial(kernel, n_slab, n_det), out_shape=pltpu....  24.3 us
    unnamed x1, local copies, waits for them, and re-layouts  0.71 us

profile of v1, /device:TPU:0, one launch (start us, length us, event | category | flops | bytes accessed | tf_op | source)
XLA Modules:
  0.0 25.1 jit_solution(8609437943306649121)
XLA Ops:
  0.0 24.3 %shard_map.55 = f32[128,512]{1,0:T(8,128)S(1)} custom-call(f32[1,128,4096]{2,1,0:T(8,128)} %traces.1, bf16[4,256,512]{2,1,0:T(8,128)(2,1)} %tables.1, s32[1,2]{1,0:T(1,128)} %slab_range.1, s32[1,7]{1,0:T(1,128)} %table_slot.1, s32[1,7]{1,0:T(1,128)} %sample_start.1), custom_call_target="tpu_custom_call" | custom-call | tf_op jit(solution)/shard_map/pallas_call | solution.py:270
  24.4 0.7 %copy.7 = f32[128,512]{1,0:T(8,128)} copy(f32[128,512]{1,0:T(8,128)S(1)} %shard_map.55) | data formatting | bytes 524288

commit v2 on v1

--- a/solution.py
+++ b/solution.py
@@ -12,11 +12,10 @@
 NTAB = 4
 RANGE = 3
 LANES = 128
+SUBLANES = 8
 OFFSETS = 2 * RANGE + 1
 ROWS = 16
 LAG = 4
-WORK = jnp.float32
-BITS = (1, 2, 4, 8, 16, 32, 64)
 AWAY = [o for o in range(OFFSETS) if o != RANGE]
 
 
@@ -32,7 +31,7 @@
     *trace_bufs,
 ):
     slab, det = lax.axis_index("slab"), lax.axis_index("det")
-    n_chunk = send_win.shape[0]
+    n_chunk = got_win.shape[0]
     half = n_det // 2
 
     smalls = [
@@ -43,12 +42,11 @@
     ]
     for copy in smalls:
         copy.start()
-
-    def rows_of(c):
-        return pl.ds(c * ROWS, ROWS)
-
+    groups = ROWS // SUBLANES
     loads = [
-        pltpu.make_async_copy(traces.at[0, rows_of(c)], trace_bufs[c], trace_sem.at[c])
+        pltpu.make_async_copy(
+            traces.at[pl.ds(c * groups, groups)], trace_bufs[c], trace_sem.at[c]
+        )
         for c in range(n_chunk)
     ]
     for copy in loads:
@@ -64,15 +62,16 @@
     outer = jnp.where(left, det - 1, det + 1)
 
     barrier = pltpu.get_barrier_semaphore()
-    peers = jnp.int32(0)
+    partners = jnp.int32(0)
     for o in AWAY:
         peer = slab + (o - RANGE)
-        peers = peers + valid(peer).astype(jnp.int32)
+        partners = partners + valid(peer).astype(jnp.int32)
 
         @pl.when(valid(peer))
         def _():
             pl.semaphore_signal(barrier, 1, device_id=(peer, det), device_id_type=MESH)
 
+    peers = partners
     for step in (-1, 1):
         near = det + step
         there = (near >= 0) & (near < n_det)
@@ -90,41 +89,45 @@
             for c in range(n_chunk):
                 got_win[c, o] = jnp.zeros(got_win.shape[2:], got_win.dtype)
 
-    def mask_copy(o):
+    def mask_copy(o, n=None):
+        at = o if n is None else pl.ds(o, n)
         return pltpu.make_async_remote_copy(
-            src_ref=send_mask.at[o], dst_ref=got_mask.at[o],
-            send_sem=mask_send.at[o], recv_sem=mask_recv.at[o],
+            src_ref=send_mask.at[at], dst_ref=got_mask.at[at],
+            send_sem=mask_send, recv_sem=mask_recv,
             device_id=(slab + (o - RANGE), det), device_id_type=MESH,
         )
 
     def win_copy(c, o):
         return pltpu.make_async_remote_copy(
-            src_ref=send_win.at[c, o], dst_ref=got_win.at[c, o],
-            send_sem=win_send.at[c, o], recv_sem=win_recv.at[c, o],
+            src_ref=send_win.at[o, c], dst_ref=got_win.at[c, o],
+            send_sem=win_send.at[o], recv_sem=win_recv.at[c],
             device_id=(slab + (o - RANGE), det), device_id_type=MESH,
         )
 
     def up_copy(c, cross):
         return pltpu.make_async_remote_copy(
             src_ref=up.at[c], dst_ref=(from_inner if cross else from_outer).at[c],
-            send_sem=up_send.at[c], recv_sem=(inner_recv if cross else outer_recv).at[c],
+            send_sem=up_send, recv_sem=(inner_recv if cross else outer_recv).at[c],
             device_id=(slab, inner), device_id_type=MESH,
         )
 
     def down_copy(c):
         return pltpu.make_async_remote_copy(
             src_ref=down.at[c], dst_ref=from_inner.at[c],
-            send_sem=down_send.at[c], recv_sem=inner_recv.at[c],
+            send_sem=down_send, recv_sem=inner_recv.at[c],
             device_id=(slab, outer), device_id_type=MESH,
         )
+
+    def per_partners(wait):
+        for n in range(1, OFFSETS):
+            pl.when(partners == n)(functools.partial(wait, n))
 
     for copy in smalls:
         copy.wait()
-    n_tile = traces.shape[2] // LANES
-    steps = [1 << b for b in reversed(range((n_tile - 1).bit_length()))]
-    lane = lax.broadcasted_iota(jnp.int32, (ROWS, LANES), 1)
+    n_tile = traces.shape[1]
+    lane = lax.broadcasted_iota(jnp.int32, (SUBLANES, LANES), 1)
     mask_rows = lax.broadcasted_iota(jnp.int32, send_mask.shape[1:], 0)
-    hits, turns, keeps = [], [], []
+    firsts, backs, keeps = [], [], []
     for o in range(OFFSETS):
         target = slab + (o - RANGE)
         low, high, slot = (
@@ -133,25 +136,35 @@
         )
         hit = (low <= target) & (target <= high) & (mask_rows == slot)
         send_mask[o] = hit.astype(jnp.float32)
-        start = jnp.full(lane.shape, start_buf[0, o])
-        hits.append([(start & (step * LANES)) != 0 for step in steps])
-        turns.append([(start & bit) != 0 for bit in BITS])
-        keeps.append(lane < LANES - (start & (LANES - 1)))
+        start = start_buf[0, o]
+        firsts.append(start >> 7)
+        past = start & (LANES - 1)
+        backs.append((LANES - past) & (LANES - 1))
+        keeps.append(lane < LANES - past)
 
     def window(c, o):
-        def tile(i):
-            i = min(i, n_tile - 1)
-            return trace_bufs[c][:, i * LANES : (i + 1) * LANES].astype(WORK)
-
-        tiles = None
-        for step, hit in zip(steps, hits[o]):
-            get = tile if tiles is None else tiles.__getitem__
-            tiles = [jnp.where(hit, get(i + step), get(i)) for i in range(step + 2)]
-        for bit, hit in zip(BITS, turns[o]):
-            tiles = [jnp.where(hit, pltpu.roll(x, LANES - bit, 1), x) for x in tiles]
         for i in range(KWIN // LANES):
-            piece = jnp.where(keeps[o], tiles[i], tiles[i + 1])
-            send_win[c, o, :, i * LANES : (i + 1) * LANES] = piece.astype(jnp.bfloat16)
+            pieces = []
+            for g in range(groups):
+                x, y = (
+                    pltpu.roll(
+                        trace_bufs[c][g, jnp.minimum(firsts[o] + i + k, n_tile - 1)], backs[o], 1
+                    )
+                    for k in range(2)
+                )
+                pieces.append(jnp.where(keeps[o], x, y))
+            piece = jnp.concatenate(pieces, axis=0).astype(jnp.bfloat16)
+            send_win[o, c, :, i * LANES : (i + 1) * LANES] = piece
+
+    def send(c, parity):
+        for o in AWAY:
+            to = slab + (o - RANGE)
+
+            @pl.when(valid(to) & (lax.rem(slab + (o + OFFSETS), 2) == parity))
+            def _():
+                if c == 0:
+                    mask_copy(o).start()
+                win_copy(c, o).start()
 
     for c in range(n_chunk):
         loads[c].wait()
@@ -159,27 +172,23 @@
             window(c, o)
         if c == 0:
             pl.semaphore_wait(barrier, peers)
-        for o in AWAY:
-
-            @pl.when(valid(slab + (o - RANGE)))
-            def _():
-                if c == 0:
-                    mask_copy(o).start()
-                win_copy(c, o).start()
+        send(c, 0)
+    for c in range(n_chunk):
+        send(c, 1)
 
     def stack(c):
-        for o in AWAY:
-
-            @pl.when(valid(slab - (o - RANGE)))
-            def _():
-                if c == 0:
-                    mask_copy(o).wait_recv()
-                win_copy(c, o).wait_recv()
+        @per_partners
+        def _(n):
+            if c == 0:
+                mask_copy(0, n).wait_recv()
+            pltpu.make_async_copy(
+                got_win.at[c, pl.ds(0, n)], got_win.at[c, pl.ds(0, n)], win_recv.at[c]
+            ).wait()
 
         bins = [jnp.zeros((ROWS, KWIN), jnp.float32) for _ in range(NTAB)]
         for o in range(OFFSETS):
             if o == RANGE:
-                win, mask = send_win[c, o], send_mask
+                win, mask = send_win[o, c], send_mask
             else:
                 win, mask = got_win[c, o], got_mask
             win = win.astype(jnp.float32)
@@ -241,28 +250,31 @@
                 down_copy(c).wait_recv()
                 if c % pair == pair - 1:
                     image(from_inner, c + 1 - pair, pair)
-        for c in range(n_chunk):
-            up_copy(c, cross).wait_send()
-            if has_outer:
-                down_copy(c).wait_send()
+        for used, copied, sem in ((True, up, up_send), (has_outer, down, down_send)):
+            if used:
+                pltpu.make_async_copy(copied, copied, sem).wait()
 
     edge = (det == 0) | (det == n_det - 1)
     pl.when(edge)(lambda: role(False, False))
     pl.when(jnp.logical_not(edge))(lambda: role(True, True))
 
+    @per_partners
+    def _(n):
+        mask_copy(0, n).wait_send()
+
     for o in AWAY:
 
         @pl.when(valid(slab + (o - RANGE)))
         def _():
-            mask_copy(o).wait_send()
-            for c in range(n_chunk):
-                win_copy(c, o).wait_send()
+            pltpu.make_async_copy(send_win.at[o], send_win.at[o], win_send.at[o]).wait()
 
 
 def body(n_slab, n_det, traces, tables, slab_range, table_slot, sample_start):
     _, frames, samp = traces.shape
     voxels = tables.shape[2]
     n_chunk = frames // ROWS
+    n_tile = samp // LANES
+    tiled = traces.reshape(frames // SUBLANES, SUBLANES, n_tile, LANES).transpose(0, 2, 1, 3)
     wide = NTAB * KWIN
     mask_rows = -(-NTAB // 8) * 8
     anywhere = pl.BlockSpec(memory_space=pl.ANY)
@@ -277,7 +289,7 @@
             pltpu.SMEM(slab_range.shape, jnp.int32),
             pltpu.SMEM(table_slot.shape, jnp.int32),
             pltpu.SMEM(sample_start.shape, jnp.int32),
-            pltpu.VMEM((n_chunk, OFFSETS, ROWS, KWIN), jnp.bfloat16),
+            pltpu.VMEM((OFFSETS, n_chunk, ROWS, KWIN), jnp.bfloat16),
             pltpu.VMEM((n_chunk, OFFSETS, ROWS, KWIN), jnp.bfloat16),
             pltpu.VMEM((OFFSETS, mask_rows, LANES), jnp.float32),
             pltpu.VMEM((OFFSETS, mask_rows, LANES), jnp.float32),
@@ -289,20 +301,23 @@
             dma((n_chunk,)),
             dma,
             dma((3,)),
-            dma((n_chunk, OFFSETS)),
-            dma((n_chunk, OFFSETS)),
-            dma((OFFSETS,)),
             dma((OFFSETS,)),
             dma((n_chunk,)),
+            dma,
+            dma,
+            dma,
             dma((n_chunk,)),
+            dma,
             dma((n_chunk,)),
-            dma((n_chunk,)),
-            *[pltpu.VMEM((ROWS, samp), jnp.float32) for _ in range(n_chunk)],
+            *[
+                pltpu.VMEM((ROWS // SUBLANES, n_tile, SUBLANES, LANES), jnp.float32)
+                for _ in range(n_chunk)
+            ],
         ],
         compiler_params=pltpu.CompilerParams(
             collective_id=0, has_side_effects=True, vmem_limit_bytes=66_500_000
         ),
-    )(traces, tables, slab_range, table_slot, sample_start)
+    )(tiled, tables, slab_range, table_slot, sample_start)
 
 
 def solution(mesh):

time: 25.2 us -> 23.1 us (0.917)
  the two profiles are of different devices: /device:TPU:0 before, /device:TPU:1 now
where the time goes in v2:
time: 23.1 us; the launch traced here: 22.9 us
  Pallas kernels  22.2 us (96%)
  local copies, waits for them, and re-layouts  0.71 us (3%)
    pallas_call x1, Pallas kernels, body(): pl.pallas_call(functools.partial(kernel, n_slab, n_det), out_shape=pltpu....  22.2 us
    unnamed x1, local copies, waits for them, and re-layouts  0.71 us

profile of v2, /device:TPU:1, one launch (start us, length us, event | category | flops | bytes accessed | tf_op | source)
XLA Modules:
  0.0 22.9 jit_solution(13965957366831661571)
XLA Ops:
  0.0 22.2 %shard_map.55 = f32[128,512]{1,0:T(8,128)S(1)} custom-call(f32[16,32,8,128]{3,2,1,0:T(8,128)} %bitcast.3, bf16[4,256,512]{2,1,0:T(8,128)(2,1)} %tables.1, s32[1,2]{1,0:T(1,128)} %slab_range.1, s32[1,7]{1,0:T(1,128)} %table_slot.1, s32[1,7]{1,0:T(1,128)} %sample_start.1), custom_call_target="tpu_custom_call" | custom-call | tf_op jit(solution)/shard_map/pallas_call | solution.py:282
  22.2 0.7 %copy.7 = f32[128,512]{1,0:T(8,128)} copy(f32[128,512]{1,0:T(8,128)S(1)} %shard_map.55) | data formatting | bytes 524288

commit v3 on v2

--- a/solution.py
+++ b/solution.py
@@ -16,23 +16,31 @@
 OFFSETS = 2 * RANGE + 1
 ROWS = 16
 LAG = 4
+DIRECT = 3
+LEAD = 3
+GROUP = 2
 AWAY = [o for o in range(OFFSETS) if o != RANGE]
+
+
+def n_far_of(n_det, n_chunk):
+    return min(DIRECT, n_chunk) if n_det > 3 else 0
 
 
 def kernel(
     n_slab, n_det,
     traces, tables, slab_range, table_slot, sample_start, out,
     table_buf, range_buf, slot_buf, start_buf,
-    send_win, got_win, send_mask, got_mask,
+    send_win, got_win, far_win, send_mask, got_mask, far_mask,
     own, up, from_outer, from_inner, down,
     trace_sem, table_sem, small_sem,
-    win_send, win_recv, mask_send, mask_recv,
+    win_send, win_recv, far_recv, mask_send, mask_recv, far_mask_send, far_mask_recv,
     up_send, outer_recv, down_send, inner_recv,
     *trace_bufs,
 ):
     slab, det = lax.axis_index("slab"), lax.axis_index("det")
     n_chunk = got_win.shape[0]
-    half = n_det // 2
+    n_far = n_far_of(n_det, n_chunk)
+    half = max(n_det // 2, 1)
 
     smalls = [
         pltpu.make_async_copy(src, dst, small_sem.at[i])
@@ -71,13 +79,29 @@
         def _():
             pl.semaphore_signal(barrier, 1, device_id=(peer, det), device_id_type=MESH)
 
+    edge = (det == 0) | (det == n_det - 1)
+    beside = (det == 1) | (det == n_det - 2)
     peers = partners
+    if n_far:
+        peers = peers + jnp.where(edge, partners, 0)
+        for o in AWAY:
+            peer = slab + (o - RANGE)
+
+            @pl.when(valid(peer) & beside)
+            def _():
+                pl.semaphore_signal(barrier, 1, device_id=(peer, outer), device_id_type=MESH)
+
     for step in (-1, 1):
         near = det + step
         there = (near >= 0) & (near < n_det)
-        peers = peers + there.astype(jnp.int32)
-
-        @pl.when(there)
+        told = there
+        heard = there
+        if n_far:
+            told = there & jnp.logical_not(edge)
+            heard = there & (near > 0) & (near < n_det - 1)
+        peers = peers + heard.astype(jnp.int32)
+
+        @pl.when(told)
         def _():
             pl.semaphore_signal(barrier, 1, device_id=(slab, near), device_id_type=MESH)
 
@@ -85,7 +109,11 @@
 
         @pl.when(jnp.logical_not(valid(slab - (o - RANGE))))
         def _():
-            got_mask[o] = jnp.zeros(got_mask.shape[1:], got_mask.dtype)
+            got_mask[o] = jnp.full(got_mask.shape[1:], -1, got_mask.dtype)
+            if n_far:
+                far_mask[o] = jnp.full(far_mask.shape[1:], -1, far_mask.dtype)
+            for c in range(n_far):
+                far_win[c, o] = jnp.zeros(far_win.shape[2:], far_win.dtype)
             for c in range(n_chunk):
                 got_win[c, o] = jnp.zeros(got_win.shape[2:], got_win.dtype)
 
@@ -104,6 +132,21 @@
             device_id=(slab + (o - RANGE), det), device_id_type=MESH,
         )
 
+    def far_mask_copy(o, n=None):
+        at = o if n is None else pl.ds(o, n)
+        return pltpu.make_async_remote_copy(
+            src_ref=send_mask.at[at], dst_ref=far_mask.at[at],
+            send_sem=far_mask_send, recv_sem=far_mask_recv,
+            device_id=(slab + (o - RANGE), inner), device_id_type=MESH,
+        )
+
+    def far_copy(c, o):
+        return pltpu.make_async_remote_copy(
+            src_ref=send_win.at[o, c], dst_ref=far_win.at[c, o],
+            send_sem=win_send.at[o], recv_sem=far_recv.at[c],
+            device_id=(slab + (o - RANGE), inner), device_id_type=MESH,
+        )
+
     def up_copy(c, cross):
         return pltpu.make_async_remote_copy(
             src_ref=up.at[c], dst_ref=(from_inner if cross else from_outer).at[c],
@@ -119,23 +162,22 @@
         )
 
     def per_partners(wait):
-        for n in range(1, OFFSETS):
+        for n in range(0, OFFSETS):
             pl.when(partners == n)(functools.partial(wait, n))
 
     for copy in smalls:
         copy.wait()
     n_tile = traces.shape[1]
     lane = lax.broadcasted_iota(jnp.int32, (SUBLANES, LANES), 1)
-    mask_rows = lax.broadcasted_iota(jnp.int32, send_mask.shape[1:], 0)
     firsts, backs, keeps = [], [], []
     for o in range(OFFSETS):
         target = slab + (o - RANGE)
         low, high, slot = (
-            jnp.full(mask_rows.shape, value)
+            jnp.full(send_mask.shape[1:], value)
             for value in (range_buf[0, 0], range_buf[0, 1], slot_buf[0, o])
         )
-        hit = (low <= target) & (target <= high) & (mask_rows == slot)
-        send_mask[o] = hit.astype(jnp.float32)
+        hit = (low <= target) & (target <= high)
+        send_mask[o] = jnp.where(hit, slot, -1).astype(jnp.float32)
         start = start_buf[0, o]
         firsts.append(start >> 7)
         past = start & (LANES - 1)
@@ -157,45 +199,66 @@
             send_win[o, c, :, i * LANES : (i + 1) * LANES] = piece
 
     def send(c, parity):
-        for o in AWAY:
+        for o in range(OFFSETS):
             to = slab + (o - RANGE)
-
-            @pl.when(valid(to) & (lax.rem(slab + (o + OFFSETS), 2) == parity))
-            def _():
+            now = valid(to) & (lax.rem(slab + (o + OFFSETS), 2) == parity)
+            if c < n_far:
+
+                @pl.when(now & edge)
+                def _():
+                    if c == 0:
+                        far_mask_copy(o).start()
+                    far_copy(c, o).start()
+
+            if o != RANGE:
+
+                @pl.when(now & jnp.logical_not(edge) if c < n_far else now)
+                def _():
+                    win_copy(c, o).start()
+
                 if c == 0:
-                    mask_copy(o).start()
-                win_copy(c, o).start()
-
-    for c in range(n_chunk):
-        loads[c].wait()
-        for o in range(OFFSETS):
-            window(c, o)
-        if c == 0:
-            pl.semaphore_wait(barrier, peers)
-        send(c, 0)
-    for c in range(n_chunk):
-        send(c, 1)
-
-    def stack(c):
+                    pl.when(now)(lambda: mask_copy(o).start())
+
+    for step in range(n_chunk + LEAD):
+        if step < n_chunk:
+            loads[step].wait()
+            for o in range(OFFSETS):
+                window(step, o)
+            if step == 0:
+                pl.semaphore_wait(barrier, peers)
+            send(step, 0)
+        if step >= LEAD:
+            send(step - LEAD, 1)
+
+    def stack(c, far):
+        wins, masks, sem = (far_win, far_mask, far_recv) if far else (got_win, got_mask, win_recv)
+
         @per_partners
         def _(n):
-            if c == 0:
-                mask_copy(0, n).wait_recv()
-            pltpu.make_async_copy(
-                got_win.at[c, pl.ds(0, n)], got_win.at[c, pl.ds(0, n)], win_recv.at[c]
-            ).wait()
+            n = n + 1 if far else n
+            if n:
+                arrived = wins.at[c, pl.ds(0, n)]
+                pltpu.make_async_copy(arrived, arrived, sem.at[c]).wait()
 
         bins = [jnp.zeros((ROWS, KWIN), jnp.float32) for _ in range(NTAB)]
         for o in range(OFFSETS):
-            if o == RANGE:
+            if o == RANGE and not far:
                 win, mask = send_win[o, c], send_mask
             else:
-                win, mask = got_win[c, o], got_mask
+                win, mask = wins[c, o], masks
             win = win.astype(jnp.float32)
+            slot = jnp.concatenate([jnp.broadcast_to(mask[o], (ROWS, LANES))] * (KWIN // LANES), axis=1)
             for t in range(NTAB):
-                weight = jnp.concatenate([mask[o, t : t + 1]] * (KWIN // LANES), axis=1)
-                bins[t] = bins[t] + weight * win
+                bins[t] = bins[t] + jnp.where(slot == t, win, 0.0)
         return bins
+
+    def wait_masks(far):
+        @per_partners
+        def _(n):
+            if far:
+                far_mask_copy(0, n + 1).wait_recv()
+            elif n:
+                mask_copy(0, n).wait_recv()
 
     def cols(t):
         return slice(t * KWIN, (t + 1) * KWIN)
@@ -209,14 +272,37 @@
             sums, weights(), preferred_element_type=jnp.float32
         )
 
-    def role(has_outer, cross):
+    def wait_sends(far):
+        @per_partners
+        def _(n):
+            if n:
+                mask_copy(0, n).wait_send()
+            if far:
+                far_mask_copy(0, n + 1).wait_send()
+
+        for o in AWAY:
+
+            @pl.when(valid(slab + (o - RANGE)))
+            def _():
+                pltpu.make_async_copy(send_win.at[o], send_win.at[o], win_send.at[o]).wait()
+
+        if far:
+            sent = send_win.at[RANGE, pl.ds(0, n_far)]
+            pltpu.make_async_copy(sent, sent, win_send.at[RANGE]).wait()
+
+    def role(has_outer, cross, gets_far):
+        gives_far = n_far > 0 and not has_outer
+
         def send_up(c):
-            bins = stack(c)
-            if has_outer:
+            far = gets_far and c < n_far
+            bins = stack(c, False)
+            if far:
+                bins = [x + y for x, y in zip(bins, stack(c, True))]
+            elif has_outer:
                 up_copy(c, False).wait_recv()
             for t in range(NTAB):
                 total = bins[t]
-                if has_outer:
+                if has_outer and not far:
                     total = total + from_outer[c, :, cols(t)].astype(jnp.float32)
                 if cross:
                     own[c, :, cols(t)] = total
@@ -231,8 +317,12 @@
                     down[c, :, cols(t)] = total.astype(jnp.bfloat16)
             else:
                 down[c] = from_inner[c]
-            down_copy(c).start()
-
+            if has_outer:
+                down_copy(c).start()
+
+        wait_masks(False)
+        if gets_far:
+            wait_masks(True)
         if has_outer or cross:
             for i in range(n_chunk + LAG):
                 if i < n_chunk:
@@ -242,41 +332,41 @@
             table_load.wait()
             image(down, 0, n_chunk)
         else:
-            for c in range(n_chunk):
+            first = n_far if gives_far else 0
+            for c in range(first, n_chunk):
                 send_up(c)
+            wait_sends(gives_far)
+            if first < n_chunk:
+                sent = up.at[pl.ds(first, n_chunk - first)]
+                pltpu.make_async_copy(sent, sent, up_send).wait()
             table_load.wait()
-            pair = 2
             for c in range(n_chunk):
                 down_copy(c).wait_recv()
-                if c % pair == pair - 1:
-                    image(from_inner, c + 1 - pair, pair)
-        for used, copied, sem in ((True, up, up_send), (has_outer, down, down_send)):
-            if used:
-                pltpu.make_async_copy(copied, copied, sem).wait()
-
-    edge = (det == 0) | (det == n_det - 1)
-    pl.when(edge)(lambda: role(False, False))
-    pl.when(jnp.logical_not(edge))(lambda: role(True, True))
-
-    @per_partners
-    def _(n):
-        mask_copy(0, n).wait_send()
-
-    for o in AWAY:
-
-        @pl.when(valid(slab + (o - RANGE)))
-        def _():
-            pltpu.make_async_copy(send_win.at[o], send_win.at[o], win_send.at[o]).wait()
+                if (c + 1) % GROUP == 0:
+                    image(from_inner, c + 1 - GROUP, GROUP)
+        if has_outer or cross:
+            wait_sends(False)
+            pltpu.make_async_copy(up, up, up_send).wait()
+            if has_outer:
+                pltpu.make_async_copy(down, down, down_send).wait()
+
+    roles = {}
+    for d in range(n_det):
+        kind = (0 < d < n_det - 1, d in (half - 1, half), n_far > 0 and d in (1, n_det - 2))
+        roles.setdefault(kind, []).append(d)
+    for kind, members in roles.items():
+        here = functools.reduce(jnp.logical_or, [det == d for d in members])
+        pl.when(here)(functools.partial(role, *kind))
 
 
 def body(n_slab, n_det, traces, tables, slab_range, table_slot, sample_start):
     _, frames, samp = traces.shape
     voxels = tables.shape[2]
     n_chunk = frames // ROWS
+    n_far = n_far_of(n_det, n_chunk)
     n_tile = samp // LANES
     tiled = traces.reshape(frames // SUBLANES, SUBLANES, n_tile, LANES).transpose(0, 2, 1, 3)
     wide = NTAB * KWIN
-    mask_rows = -(-NTAB // 8) * 8
     anywhere = pl.BlockSpec(memory_space=pl.ANY)
     dma = pltpu.SemaphoreType.DMA
     return pl.pallas_call(
@@ -291,8 +381,10 @@
             pltpu.SMEM(sample_start.shape, jnp.int32),
             pltpu.VMEM((OFFSETS, n_chunk, ROWS, KWIN), jnp.bfloat16),
             pltpu.VMEM((n_chunk, OFFSETS, ROWS, KWIN), jnp.bfloat16),
-            pltpu.VMEM((OFFSETS, mask_rows, LANES), jnp.float32),
-            pltpu.VMEM((OFFSETS, mask_rows, LANES), jnp.float32),
+            pltpu.VMEM((max(n_far, 1), OFFSETS, ROWS, KWIN), jnp.bfloat16),
+            pltpu.VMEM((OFFSETS, 1, LANES), jnp.float32),
+            pltpu.VMEM((OFFSETS, 1, LANES), jnp.float32),
+            pltpu.VMEM((OFFSETS, 1, LANES), jnp.float32),
             pltpu.VMEM((n_chunk, ROWS, wide), jnp.float32),
             pltpu.VMEM((n_chunk, ROWS, wide), jnp.bfloat16),
             pltpu.VMEM((n_chunk, ROWS, wide), jnp.bfloat16),
@@ -303,6 +395,9 @@
             dma((3,)),
             dma((OFFSETS,)),
             dma((n_chunk,)),
+            dma((max(n_far, 1),)),
+            dma,
+            dma,
             dma,
             dma,
             dma,

time: 23.1 us -> 22.1 us (0.957)
  the two profiles are of different devices: /device:TPU:1 before, /device:TPU:0 now
where the time goes in v3:
time: 22.1 us; the launch traced here: 21.9 us
  Pallas kernels  21.2 us (96%)
  local copies, waits for them, and re-layouts  0.71 us (3%)
    pallas_call x1, Pallas kernels, body(): pl.pallas_call(functools.partial(kernel, n_slab, n_det), out_shape=pltpu....  21.2 us
    unnamed x1, local copies, waits for them, and re-layouts  0.71 us

profile of v3, /device:TPU:0, one launch (start us, length us, event | category | flops | bytes accessed | tf_op | source)
XLA Modules:
  0.0 21.9 jit_solution(12092456985804419298)
XLA Ops:
  0.0 21.2 %shard_map.55 = f32[128,512]{1,0:T(8,128)S(1)} custom-call(f32[16,32,8,128]{3,2,1,0:T(8,128)} %bitcast.3, bf16[4,256,512]{2,1,0:T(8,128)(2,1)} %tables.1, s32[1,2]{1,0:T(1,128)} %slab_range.1, s32[1,7]{1,0:T(1,128)} %table_slot.1, s32[1,7]{1,0:T(1,128)} %sample_start.1), custom_call_target="tpu_custom_call" | custom-call | tf_op jit(solution)/shard_map/pallas_call | solution.py:372
  21.2 0.7 %copy.7 = f32[128,512]{1,0:T(8,128)} copy(f32[128,512]{1,0:T(8,128)S(1)} %shard_map.55) | data formatting | bytes 524288

commit v4 on v2

v4 whole, which is shorter than its diff:
```python
import functools

import jax
import jax.numpy as jnp
from jax import lax
from jax.experimental import pallas as pl
from jax.experimental.pallas import tpu as pltpu
from jax.sharding import PartitionSpec as P

MESH = pl.DeviceIdType.MESH
KWIN = 256
NTAB = 4
RANGE = 3
LANES = 128
SUBLANES = 8
OFFSETS = 2 * RANGE + 1
ROWS = 16
LAG = 7
DIRECT = 3
LEAD = 0
GROUP = 2
GROUPS = ROWS // SUBLANES


def sizes(n_slab, n_det, frames):
    pair = 2 if n_slab % 2 == 0 else 1
    n_chunk = frames // ROWS
    return pair, n_chunk, min(DIRECT, n_chunk) if n_det == 4 else 0


def kernel(
    n_slab, n_det,
    traces, tables, slab_range, table_slot, sample_start, out,
    first_buf, rest_buf, table_buf, range_buf, slot_buf, start_buf,
    send_win, got_win, far_win, send_mask, got_mask, far_mask,
    own, up, from_outer, from_inner, down,
    trace_sem, table_sem, small_sem,
    win_send, far_send, win_recv, mask_send, mask_recv, far_mask_send, far_mask_recv,
    up_send, outer_recv, down_send, client_send, inner_recv,
):
    slab, det = lax.axis_index("slab"), lax.axis_index("det")
    pair, n_chunk, n_far = sizes(n_slab, n_det, out.shape[0])
    half = n_det // 2

    smalls = [
        pltpu.make_async_copy(src, dst, small_sem.at[i])
        for i, (src, dst) in enumerate(
            [(sample_start, start_buf), (slab_range, range_buf), (table_slot, slot_buf)]
        )
    ]
    for copy in smalls:
        copy.start()
    loads = [
        pltpu.make_async_copy(traces.at[pl.ds(0, GROUPS)], first_buf, trace_sem.at[0]),
        pltpu.make_async_copy(
            traces.at[pl.ds(GROUPS, rest_buf.shape[0])], rest_buf, trace_sem.at[1]
        ),
    ]
    for copy in loads:
        copy.start()

    def valid(to):
        return (to >= 0) & (to < n_slab)

    def place(to):
        return lax.rem(to + pair * OFFSETS, pair)

    def hosts(to):
        return place(to) == pair - 1

    is_host = hosts(slab)
    host = slab - place(slab) + (pair - 1)
    left = det < half
    inner = jnp.where(left, det + 1, det - 1)
    outer = jnp.where(left, det - 1, det + 1)
    edge = (det == 0) | (det == n_det - 1)
    middle = (det == half - 1) | (det == half)

    def member(p):
        return host - (pair - 1) + p

    def sources(to):
        return jnp.minimum(to, RANGE) + jnp.minimum(n_slab - 1 - to, RANGE)

    source_counts = sorted({min(t, RANGE) + min(n_slab - 1 - t, RANGE) for t in range(n_slab)})

    def per_count(count, options, act):
        for n in options:
            pl.when(count == n)(functools.partial(act, n))

    barrier = pltpu.get_barrier_semaphore()
    heard = jnp.int32(0)

    def tell(condition, to, at):
        @pl.when(condition)
        def _():
            pl.semaphore_signal(barrier, 1, device_id=(to, at), device_id_type=MESH)

    for k in range(-RANGE, RANGE + pair):
        source, target = slab - k, slab + k
        writes = valid(target) & hosts(target)
        if k:
            tell(is_host & valid(source), source, det)
            heard = heard + writes.astype(jnp.int32)
        if n_far:
            tell(is_host & middle & valid(source), source, outer)
            heard = heard + (writes & edge).astype(jnp.int32)
    if n_far:
        tell(is_host & middle, slab, inner)
        heard = heard + (is_host & middle).astype(jnp.int32)
    else:
        for step in (-1, 1):
            near = det + step
            there = (near >= 0) & (near < n_det)
            for p in range(pair):
                tell(there & (is_host | (p == pair - 1)), member(p), near)
            heard = heard + jnp.where(there, jnp.where(is_host, pair, 1), 0)

    table_load = pltpu.make_async_copy(tables, table_buf, table_sem)
    table_load.start()

    for p in range(pair):
        for o in range(OFFSETS):

            @pl.when(is_host & jnp.logical_not(valid(member(p) - (o - RANGE))))
            def _():
                got_mask[p, o] = jnp.full(got_mask.shape[2:], -1, got_mask.dtype)
                far_mask[p, o] = jnp.full(far_mask.shape[2:], -1, far_mask.dtype)
                for c in range(n_chunk):
                    got_win[c, p, o] = jnp.zeros(got_win.shape[3:], got_win.dtype)
                for c in range(n_far):
                    far_win[c, p, o] = jnp.zeros(far_win.shape[3:], far_win.dtype)

    def send_copy(src, dst, to, at, sent, landed):
        return pltpu.make_async_remote_copy(
            src_ref=src, dst_ref=dst, send_sem=sent, recv_sem=landed,
            device_id=(to, at), device_id_type=MESH,
        )

    def await_bytes(ref, sem):
        pltpu.make_async_copy(ref, ref, sem).wait()

    def up_copy(c, p, cross):
        into, landed = (from_inner, inner_recv) if cross else (from_outer, outer_recv)
        return send_copy(up.at[c, p], into.at[c, p], slab, inner, up_send, landed.at[c, p])

    def down_copy(c, p):
        return send_copy(
            down.at[c, p], from_inner.at[c, p], member(p), outer, down_send, inner_recv.at[c, p]
        )

    def client_copy(c, p):
        return send_copy(
            down.at[c, p], from_inner.at[c, p], member(p), det, client_send, inner_recv.at[c, p]
        )

    for copy in smalls:
        copy.wait()
    n_tile = traces.shape[1]
    lane = lax.broadcasted_iota(jnp.int32, (SUBLANES, LANES), 1)
    firsts, backs, keeps = [], [], []
    for o in range(OFFSETS):
        target = slab + (o - RANGE)
        low, high, slot = (
            jnp.full(send_mask.shape[1:], value)
            for value in (range_buf[0, 0], range_buf[0, 1], slot_buf[0, o])
        )
        hit = (low <= target) & (target <= high)
        send_mask[o] = jnp.where(hit, slot, -1).astype(jnp.float32)
        start = start_buf[0, o]
        firsts.append(start >> 7)
        past = start & (LANES - 1)
        backs.append((LANES - past) & (LANES - 1))
        keeps.append(lane < LANES - past)

    def window(c, o):
        buf, base = (first_buf, 0) if c == 0 else (rest_buf, (c - 1) * GROUPS)
        for i in range(KWIN // LANES):
            pieces = []
            for g in range(GROUPS):
                x, y = (
                    pltpu.roll(
                        buf[base + g, jnp.minimum(firsts[o] + i + k, n_tile - 1)], backs[o], 1
                    )
                    for k in range(2)
                )
                pieces.append(jnp.where(keeps[o], x, y))
            piece = jnp.concatenate(pieces, axis=0).astype(jnp.bfloat16)
            send_win[o, c, :, i * LANES : (i + 1) * LANES] = piece

    def send(c, p):
        for o in range(OFFSETS):
            to = slab + (o - RANGE)
            at = to - p + (pair - 1)
            now = valid(to) & (place(to) == p)
            away = now & (at != slab)
            if c < n_far:

                @pl.when(now & edge)
                def _():
                    if c == 0:
                        send_copy(
                            send_mask.at[o], far_mask.at[p, o], at, inner,
                            far_mask_send, far_mask_recv.at[p],
                        ).start()
                    send_copy(
                        send_win.at[o, c], far_win.at[c, p, o], at, inner,
                        far_send, outer_recv.at[c, p],
                    ).start()

            @pl.when(away & jnp.logical_not(edge) if c < n_far else away)
            def _():
                send_copy(
                    send_win.at[o, c], got_win.at[c, p, o], at, det, win_send, win_recv.at[c, p]
                ).start()

            if c == 0:

                @pl.when(away)
                def _():
                    send_copy(
                        send_mask.at[o], got_mask.at[p, o], at, det, mask_send, mask_recv.at[p]
                    ).start()

    for step in range(n_chunk + LEAD):
        if step < n_chunk:
            if step < len(loads):
                loads[step].wait()
            for o in range(OFFSETS):
                window(step, o)
            if step == 0:
                pl.semaphore_wait(barrier, heard)
            send(step, 0)
        if step >= LEAD:
            for p in range(1, pair):
                send(step - LEAD, p)

    def stack(c, p, far):
        wins, masks, sem = (
            (far_win, far_mask, outer_recv) if far else (got_win, got_mask, win_recv)
        )

        def arrive(n):
            n = n + 1 if far else n
            if n:
                arrived = wins.at[c, p, pl.ds(0, n)]
                await_bytes(arrived, sem.at[c, p])

        per_count(sources(member(p)), source_counts, arrive)
        mine = None if far else RANGE - (pair - 1) + p
        bins = [jnp.zeros((ROWS, KWIN), jnp.float32) for _ in range(NTAB)]
        for o in range(OFFSETS):
            if o == mine:
                win, mask = send_win[o, c], send_mask[o]
            else:
                win, mask = wins[c, p, o], masks[p, o]
            win = win.astype(jnp.float32)
            slot = jnp.broadcast_to(mask, (ROWS, LANES))
            slot = jnp.concatenate([slot] * (KWIN // LANES), axis=1)
            for t in range(NTAB):
                bins[t] = bins[t] + jnp.where(slot == t, win, 0.0)
        return bins

    def wait_masks(masks, sem, extra):
        for p in range(pair):

            def arrive(n):
                if n + extra:
                    await_bytes(masks.at[p, pl.ds(0, n + extra)], sem.at[p])

            per_count(sources(member(p)), source_counts, arrive)

    def cols(t):
        return slice(t * KWIN, (t + 1) * KWIN)

    def image(ref, p, c, n):
        sums = ref[c : c + n, p].reshape(n * ROWS, NTAB * KWIN)
        weights = table_buf[...].reshape(NTAB * KWIN, table_buf.shape[2])
        out[c * ROWS : (c + n) * ROWS] = jnp.dot(
            sums, weights, preferred_element_type=jnp.float32
        )

    def wait_sends(hosting, far):
        local = pair if hosting else 0

        def sent(n):
            n = n + 1
            if n > local:
                chunks = pl.ds(far, n_chunk - far)
                if far < n_chunk:
                    await_bytes(send_win.at[pl.ds(0, n - local), chunks], win_send)
                await_bytes(send_mask.at[pl.ds(0, n - local)], mask_send)
            if far:
                await_bytes(send_win.at[pl.ds(0, n), pl.ds(0, far)], far_send)
                await_bytes(send_mask.at[pl.ds(0, n)], far_mask_send)

        per_count(sources(slab), source_counts, sent)

    def finish(p):
        table_load.wait()
        for c in range(n_chunk):
            await_bytes(from_inner.at[c, p], inner_recv.at[c, p])
            if (c + 1) % GROUP == 0 or c == n_chunk - 1:
                image(from_inner, p, c - c % GROUP, c % GROUP + 1)

    def role_host(has_outer, cross, gets_far):
        gives_far = n_far if not has_outer and not cross else 0

        def send_up(c, p):
            far = gets_far and c < n_far
            bins = stack(c, p, False)
            if far:
                bins = [x + y for x, y in zip(bins, stack(c, p, True))]
            elif has_outer:
                await_bytes(from_outer.at[c, p], outer_recv.at[c, p])
            for t in range(NTAB):
                total = bins[t]
                if has_outer and not far:
                    total = total + from_outer[c, p, :, cols(t)].astype(jnp.float32)
                if cross:
                    own[c, p, :, cols(t)] = total
                up[c, p, :, cols(t)] = total.astype(jnp.bfloat16)
            up_copy(c, p, cross).start()

        def send_down(c, p):
            await_bytes(from_inner.at[c, p], inner_recv.at[c, p])
            for t in range(NTAB):
                total = own[c, p, :, cols(t)] + from_inner[c, p, :, cols(t)].astype(jnp.float32)
                down[c, p, :, cols(t)] = total.astype(jnp.bfloat16)
            if has_outer:
                down_copy(c, p).start()
            if p < pair - 1:
                client_copy(c, p).start()

        tasks = [(c, p) for c in range(n_chunk) for p in range(pair)]
        wait_masks(got_mask, mask_recv, 0)
        if gets_far:
            wait_masks(far_mask, far_mask_recv, 1)
        if cross:
            for i in range(len(tasks) + LAG):
                if i < len(tasks):
                    send_up(*tasks[i])
                if i >= LAG:
                    send_down(*tasks[i - LAG])
            table_load.wait()
            image(down, pair - 1, 0, n_chunk)
            wait_sends(True, 0)
            await_bytes(up, up_send)
            if has_outer:
                await_bytes(down, down_send)
            if pair > 1:
                await_bytes(down.at[:, pl.ds(0, pair - 1)], client_send)
        else:
            for c, p in tasks:
                if c >= gives_far:
                    send_up(c, p)
            wait_sends(True, gives_far)
            if gives_far < n_chunk:
                await_bytes(up.at[pl.ds(gives_far, n_chunk - gives_far)], up_send)
            finish(pair - 1)

    def role_client(p, far):
        wait_sends(False, far)
        finish(p)

    kinds = {}
    for d in range(n_det):
        kind = (0 < d < n_det - 1, d in (half - 1, half), n_far > 0 and d in (1, n_det - 2))
        kinds.setdefault(kind, []).append(d)
    for kind, members in kinds.items():
        here = functools.reduce(jnp.logical_or, [det == d for d in members])
        pl.when(here & is_host)(functools.partial(role_host, *kind))
        for p in range(pair - 1):
            far = 0 if kind[0] or kind[1] else n_far
            pl.when(here & (place(slab) == p))(functools.partial(role_client, p, far))


def body(n_slab, n_det, traces, tables, slab_range, table_slot, sample_start):
    _, frames, samp = traces.shape
    voxels = tables.shape[2]
    pair, n_chunk, n_far = sizes(n_slab, n_det, frames)
    n_tile = samp // LANES
    tiled = traces.reshape(frames // SUBLANES, SUBLANES, n_tile, LANES).transpose(0, 2, 1, 3)
    wide = NTAB * KWIN
    anywhere = pl.BlockSpec(memory_space=pl.ANY)
    dma = pltpu.SemaphoreType.DMA
    bf16, f32 = jnp.bfloat16, jnp.float32
    return pl.pallas_call(
        functools.partial(kernel, n_slab, n_det),
        out_shape=pltpu.VMEM((frames, voxels), f32),
        in_specs=[anywhere] * 5,
        out_specs=pl.BlockSpec(memory_space=pltpu.VMEM),
        scratch_shapes=[
            pltpu.VMEM((GROUPS, n_tile, SUBLANES, LANES), f32),
            pltpu.VMEM((frames // SUBLANES - GROUPS, n_tile, SUBLANES, LANES), f32),
            pltpu.VMEM(tables.shape, bf16),
            pltpu.SMEM(slab_range.shape, jnp.int32),
            pltpu.SMEM(table_slot.shape, jnp.int32),
            pltpu.SMEM(sample_start.shape, jnp.int32),
            pltpu.VMEM((OFFSETS, n_chunk, ROWS, KWIN), bf16),
            pltpu.VMEM((n_chunk, pair, OFFSETS, ROWS, KWIN), bf16),
            pltpu.VMEM((max(n_far, 1), pair, OFFSETS, ROWS, KWIN), bf16),
            pltpu.VMEM((OFFSETS, 1, LANES), f32),
            pltpu.VMEM((pair, OFFSETS, 1, LANES), f32),
            pltpu.VMEM((pair, OFFSETS, 1, LANES), f32),
            pltpu.VMEM((n_chunk, pair, ROWS, wide), f32),
            pltpu.VMEM((n_chunk, pair, ROWS, wide), bf16),
            pltpu.VMEM((n_chunk, pair, ROWS, wide), bf16),
            pltpu.VMEM((n_chunk, pair, ROWS, wide), bf16),
            pltpu.VMEM((n_chunk, pair, ROWS, wide), bf16),
            dma((2,)),
            dma,
            dma((3,)),
            dma,
            dma,
            dma((n_chunk, pair)),
            dma,
            dma((pair,)),
            dma,
            dma((pair,)),
            dma,
            dma((n_chunk, pair)),
            dma,
            dma,
            dma((n_chunk, pair)),
        ],
        compiler_params=pltpu.CompilerParams(
            collective_id=0, has_side_effects=True, vmem_limit_bytes=66_500_000
        ),
    )(tiled, tables, slab_range, table_slot, sample_start)


def solution(mesh):
    placed = (
        P(("slab", "det"), None, None),
        P("slab", None, "det"),
        P(("slab", "det"), None),
        P(("slab", "det"), None),
        P(("slab", "det"), None),
    )
    return jax.shard_map(
        functools.partial(body, mesh.shape["slab"], mesh.shape["det"]),
        mesh=mesh, in_specs=placed, out_specs=P(None, ("slab", "det")), check_vma=False,
    )
```

time: 23.1 us -> 19.9 us (0.86)
  the two profiles are of different devices: /device:TPU:1 before, /device:TPU:0 now
where the time goes in v4:
time: 19.9 us; the launch traced here: 19.8 us
  Pallas kernels  19 us (95%)
  local copies, waits for them, and re-layouts  0.71 us (4%)
    pallas_call x1, Pallas kernels, body(): pl.pallas_call(functools.partial(kernel, n_slab, n_det), out_shape=pltpu....  19 us
    unnamed x1, local copies, waits for them, and re-layouts  0.71 us

profile of v4, /device:TPU:0, one launch (start us, length us, event | category | flops | bytes accessed | tf_op | source)
XLA Modules:
  0.0 19.8 jit_solution(13352808505205946396)
XLA Ops:
  0.0 19.0 %shard_map.55 = f32[128,512]{1,0:T(8,128)S(1)} custom-call(f32[16,32,8,128]{3,2,1,0:T(8,128)} %bitcast.3, bf16[4,256,512]{2,1,0:T(8,128)(2,1)} %tables.1, s32[1,2]{1,0:T(1,128)} %slab_range.1, s32[1,7]{1,0:T(1,128)} %table_slot.1, s32[1,7]{1,0:T(1,128)} %sample_start.1), custom_call_target="tpu_custom_call" | custom-call | tf_op jit(solution)/shard_map/pallas_call | solution.py:388
  19.0 0.7 %copy.7 = f32[128,512]{1,0:T(8,128)} copy(f32[128,512]{1,0:T(8,128)S(1)} %shard_map.55) | data formatting | bytes 524288

commit v5 on v4

v5 whole, which is shorter than its diff:
```python
import functools

import jax
import jax.numpy as jnp
from jax import lax
from jax.experimental import pallas as pl
from jax.experimental.pallas import tpu as pltpu
from jax.sharding import PartitionSpec as P

MESH = pl.DeviceIdType.MESH
KWIN = 256
NTAB = 4
RANGE = 3
LANES = 128
SUBLANES = 8
OFFSETS = 2 * RANGE + 1
ROWS = 16
LAG = 5
DIRECT = 2
SKIP = 0
AHEAD = 1
DOT = 32


def sizes(n_slab, n_det, frames):
    pair = 2 if n_slab % 2 == 0 else 1
    n_chunk = frames // ROWS
    far = range(SKIP, min(SKIP + DIRECT, n_chunk)) if n_det == 4 else range(0)
    return pair, n_chunk, far


def kernel(
    n_slab, n_det,
    traces, tables, slab_range, table_slot, sample_start, out,
    first_buf, rest_buf, table_buf, range_buf, slot_buf, start_buf,
    send_win, got_win, far_win, send_mask, got_mask, far_mask,
    own, up, from_outer, from_inner, down,
    trace_sem, table_sem, small_sem,
    win_send, far_send, win_recv, mask_send, mask_recv, far_mask_send, far_mask_recv,
    up_send, outer_recv, down_send, client_send, inner_recv,
):
    slab, det = lax.axis_index("slab"), lax.axis_index("det")
    frames = out.shape[0]
    pair, n_chunk, far_chunks = sizes(n_slab, n_det, frames)
    far_rows = len(far_chunks) * ROWS
    near_chunks = [c for c in range(n_chunk) if c not in far_chunks]
    order = [*far_chunks, *near_chunks]
    ahead = near_chunks[:AHEAD]
    edge_order = [*ahead, *far_chunks, *near_chunks[len(ahead) :]]
    half = n_det // 2

    edge = (det == 0) | (det == n_det - 1)

    def at_step(k):
        return k if edge_order[k] == order[k] else jnp.where(edge, edge_order[k], order[k])

    smalls = [
        pltpu.make_async_copy(src, dst, small_sem.at[i])
        for i, (src, dst) in enumerate(
            [(sample_start, start_buf), (slab_range, range_buf), (table_slot, slot_buf)]
        )
    ]
    for copy in smalls:
        copy.start()
    groups = ROWS // SUBLANES
    loads = [
        pltpu.make_async_copy(
            traces.at[pl.ds(at_step(0) * groups, groups)], first_buf, trace_sem.at[0]
        ),
        pltpu.make_async_copy(traces, rest_buf, trace_sem.at[1]),
    ]
    for copy in loads:
        copy.start()

    def valid(to):
        return (to >= 0) & (to < n_slab)

    def place(to):
        return lax.rem(to + pair * OFFSETS, pair)

    def hosts(to):
        return place(to) == pair - 1

    is_host = hosts(slab)
    host = slab - place(slab) + (pair - 1)
    left = det < half
    inner = jnp.where(left, det + 1, det - 1)
    outer = jnp.where(left, det - 1, det + 1)
    middle = (det == half - 1) | (det == half)

    def member(p):
        return host - (pair - 1) + p

    def sources(to):
        return jnp.minimum(to, RANGE) + jnp.minimum(n_slab - 1 - to, RANGE)

    source_counts = sorted({min(t, RANGE) + min(n_slab - 1 - t, RANGE) for t in range(n_slab)})

    def per_count(count, options, act):
        for n in options:
            pl.when(count == n)(functools.partial(act, n))

    barrier = pltpu.get_barrier_semaphore()
    heard = jnp.int32(0)

    def tell(condition, to, at):
        @pl.when(condition)
        def _():
            pl.semaphore_signal(barrier, 1, device_id=(to, at), device_id_type=MESH)

    for k in range(-RANGE, RANGE + pair):
        source, target = slab - k, slab + k
        writes = valid(target) & hosts(target)
        if k:
            tell(is_host & valid(source), source, det)
            heard = heard + writes.astype(jnp.int32)
        if far_rows:
            tell(is_host & middle & valid(source), source, outer)
            heard = heard + (writes & edge).astype(jnp.int32)
    if far_rows:
        tell(is_host & middle, slab, inner)
        heard = heard + (is_host & middle).astype(jnp.int32)
    else:
        for step in (-1, 1):
            near = det + step
            there = (near >= 0) & (near < n_det)
            for p in range(pair):
                tell(there & (is_host | (p == pair - 1)), member(p), near)
            heard = heard + jnp.where(there, jnp.where(is_host, pair, 1), 0)

    table_load = pltpu.make_async_copy(tables, table_buf, table_sem)
    table_load.start()

    for p in range(pair):
        for o in range(OFFSETS):

            @pl.when(is_host & jnp.logical_not(valid(member(p) - (o - RANGE))))
            def _():
                got_mask[p, o] = jnp.full(got_mask.shape[2:], -1, got_mask.dtype)
                far_mask[p, o] = jnp.full(far_mask.shape[2:], -1, far_mask.dtype)
                got_win[p, o] = jnp.zeros(got_win.shape[2:], got_win.dtype)
                far_win[p, o] = jnp.zeros(far_win.shape[2:], far_win.dtype)

    def send_copy(src, dst, to, at, sent, landed):
        return pltpu.make_async_remote_copy(
            src_ref=src, dst_ref=dst, send_sem=sent, recv_sem=landed,
            device_id=(to, at), device_id_type=MESH,
        )

    def await_bytes(ref, sem):
        pltpu.make_async_copy(ref, ref, sem).wait()

    def rows(c):
        return pl.ds(c * ROWS if isinstance(c, int) else pl.multiple_of(c * ROWS, ROWS), ROWS)

    def far_slot(c):
        return rows(c - far_chunks.start)

    def up_copy(c, p, cross):
        into, landed = (from_inner, inner_recv) if cross else (from_outer, outer_recv)
        return send_copy(up.at[p, rows(c)], into.at[p, rows(c)], slab, inner, up_send, landed.at[c, p])

    def down_copy(c, p):
        return send_copy(
            down.at[p, rows(c)], from_inner.at[p, rows(c)], member(p), outer, down_send, inner_recv.at[c, p]
        )

    def client_copy(c, p):
        return send_copy(
            down.at[p, rows(c)], from_inner.at[p, rows(c)], member(p), det, client_send, inner_recv.at[c, p]
        )

    for copy in smalls:
        copy.wait()
    n_tile = traces.shape[1]
    lane = lax.broadcasted_iota(jnp.int32, (SUBLANES, LANES), 1)
    firsts, backs, keeps = [], [], []
    for o in range(OFFSETS):
        target = slab + (o - RANGE)
        low, high, slot = (
            jnp.full(send_mask.shape[1:], value)
            for value in (range_buf[0, 0], range_buf[0, 1], slot_buf[0, o])
        )
        hit = (low <= target) & (target <= high)
        send_mask[o] = jnp.where(hit, slot, -1).astype(jnp.float32)
        start = start_buf[0, o]
        firsts.append(start >> 7)
        past = start & (LANES - 1)
        backs.append((LANES - past) & (LANES - 1))
        keeps.append(lane < LANES - past)

    def window(k, o):
        c = at_step(k)
        buf, base = (first_buf, 0) if k == 0 else (rest_buf, c * groups)
        for i in range(KWIN // LANES):
            pieces = []
            for g in range(groups):
                x, y = (
                    pltpu.roll(
                        buf[base + g, jnp.minimum(firsts[o] + i + n, n_tile - 1)], backs[o], 1
                    )
                    for n in range(2)
                )
                pieces.append(jnp.where(keeps[o], x, y))
            piece = jnp.concatenate(pieces, axis=0).astype(jnp.bfloat16)
            send_win[o, rows(c), i * LANES : (i + 1) * LANES] = piece

    def send(p, k=None):
        far = k is not None and edge_order[k] in far_chunks
        c = None if k is None else at_step(k)
        for o in range(OFFSETS):
            to = slab + (o - RANGE)
            at = to - p + (pair - 1)
            now = valid(to) & (place(to) == p)
            away = now & (at != slab)
            if c is None:
                src, near_dst, far_dst = send_mask.at[o], got_mask.at[p, o], far_mask.at[p, o]
                near_sems = mask_send, mask_recv.at[p]
                far_sems = far_mask_send, far_mask_recv.at[p]
            else:
                src, near_dst = send_win.at[o, rows(c)], got_win.at[p, o, rows(c)]
                near_sems = win_send, win_recv.at[c, p]
                if far:
                    far_dst = far_win.at[p, o, far_slot(edge_order[k])]
                    far_sems = far_send, outer_recv.at[edge_order[k], p]
            if far or (c is None and far_rows):
                pl.when(now & edge)(
                    lambda: send_copy(src, far_dst, at, inner, *far_sems).start()
                )
            pl.when(away & jnp.logical_not(edge) if far else away)(
                lambda: send_copy(src, near_dst, at, det, *near_sems).start()
            )

    for k in range(n_chunk):
        if k < len(loads):
            loads[k].wait()
        for o in range(OFFSETS):
            window(k, o)
        if k == 0:
            pl.semaphore_wait(barrier, heard)
            for p in range(pair):
                send(p)
        for p in range(pair):
            send(p, k)

    def stack(c, p, far):
        wins, masks, sem = (
            (far_win, far_mask, outer_recv) if far else (got_win, got_mask, win_recv)
        )

        slots = far_slot(c) if far else rows(c)

        def arrive(n):
            n = n + 1 if far else n
            if n:
                arrived = wins.at[p, pl.ds(0, n), slots]
                await_bytes(arrived, sem.at[c, p])

        per_count(sources(member(p)), source_counts, arrive)
        mine = None if far else RANGE - (pair - 1) + p
        bins = [jnp.zeros((ROWS, KWIN), jnp.float32) for _ in range(NTAB)]
        for o in range(OFFSETS):
            if o == mine:
                win, mask = send_win[o, rows(c)], send_mask[o]
            else:
                win, mask = wins[p, o, slots], masks[p, o]
            win = win.astype(jnp.float32)
            slot = jnp.broadcast_to(mask, (ROWS, LANES))
            slot = jnp.concatenate([slot] * (KWIN // LANES), axis=1)
            for t in range(NTAB):
                bins[t] = bins[t] + jnp.where(slot == t, win, 0.0)
        return bins

    def wait_masks(masks, sem, p, extra):
        def arrive(n):
            if n + extra:
                await_bytes(masks.at[p, pl.ds(0, n + extra)], sem.at[p])

        per_count(sources(member(p)), source_counts, arrive)

    def cols(t):
        return slice(t * KWIN, (t + 1) * KWIN)

    def image(ref, p, begin, end):
        weights = table_buf[...].reshape(NTAB * KWIN, table_buf.shape[2])
        out[begin:end] = jnp.dot(
            ref[p, begin:end], weights, preferred_element_type=jnp.float32
        )

    def wait_sends(hosting, far):
        local = pair if hosting else 0

        def sent(n):
            n = n + 1
            if n > local:
                if far < frames:
                    await_bytes(
                        send_win.at[pl.ds(0, n - local), pl.ds(0, frames - far)], win_send
                    )
                await_bytes(send_mask.at[pl.ds(0, n - local)], mask_send)
            if far:
                await_bytes(send_win.at[pl.ds(0, n), pl.ds(0, far)], far_send)
                await_bytes(send_mask.at[pl.ds(0, n)], far_mask_send)

        per_count(sources(slab), source_counts, sent)

    def finish(p):
        table_load.wait()
        group = []
        for c in order:
            if group and group[-1] + 1 != c:
                image(from_inner, p, group[0] * ROWS, (group[-1] + 1) * ROWS)
                group = []
            await_bytes(from_inner.at[p, rows(c)], inner_recv.at[c, p])
            group.append(c)
            if len(group) * ROWS >= DOT or c == order[-1]:
                image(from_inner, p, group[0] * ROWS, (group[-1] + 1) * ROWS)
                group = []

    def role_host(has_outer, cross, gets_far):
        gives = () if has_outer or cross else far_chunks

        def send_up(c, p):
            far = gets_far and c in far_chunks
            if c == order[0] or (gives and c == order[len(gives)]):
                wait_masks(got_mask, mask_recv, p, 0)
                if gets_far:
                    wait_masks(far_mask, far_mask_recv, p, 1)
            bins = stack(c, p, False)
            if far:
                bins = [x + y for x, y in zip(bins, stack(c, p, True))]
            elif has_outer:
                await_bytes(from_outer.at[p, rows(c)], outer_recv.at[c, p])
            for t in range(NTAB):
                total = bins[t]
                if has_outer and not far:
                    total = total + from_outer[p, rows(c), cols(t)].astype(jnp.float32)
                if cross:
                    own[p, rows(c), cols(t)] = total
                up[p, rows(c), cols(t)] = total.astype(jnp.bfloat16)
            up_copy(c, p, cross).start()

        def send_down(c, p):
            await_bytes(from_inner.at[p, rows(c)], inner_recv.at[c, p])
            for t in range(NTAB):
                total = own[p, rows(c), cols(t)] + from_inner[p, rows(c), cols(t)].astype(jnp.float32)
                down[p, rows(c), cols(t)] = total.astype(jnp.bfloat16)
            if has_outer:
                down_copy(c, p).start()
            if p < pair - 1:
                client_copy(c, p).start()

        tasks = [(c, p) for c in order for p in range(pair)]
        if cross:
            for i in range(len(tasks) + LAG):
                if i < len(tasks):
                    send_up(*tasks[i])
                if i >= LAG:
                    send_down(*tasks[i - LAG])
            table_load.wait()
            image(down, pair - 1, 0, frames)
            wait_sends(True, 0)
            await_bytes(up, up_send)
            if has_outer:
                await_bytes(down, down_send)
            if pair > 1:
                await_bytes(down.at[pl.ds(0, pair - 1)], client_send)
        else:
            for c, p in tasks:
                if c not in gives:
                    send_up(c, p)
            gone = len(gives) * ROWS
            wait_sends(True, gone)
            if gone < frames:
                await_bytes(up.at[:, pl.ds(0, frames - gone)], up_send)
            finish(pair - 1)

    def role_client(p, far):
        wait_sends(False, far)
        finish(p)

    kinds = {}
    for d in range(n_det):
        kind = (0 < d < n_det - 1, d in (half - 1, half), far_rows > 0 and d in (1, n_det - 2))
        kinds.setdefault(kind, []).append(d)
    for kind, members in kinds.items():
        here = functools.reduce(jnp.logical_or, [det == d for d in members])
        pl.when(here & is_host)(functools.partial(role_host, *kind))
        for p in range(pair - 1):
            far = 0 if kind[0] or kind[1] else far_rows
            pl.when(here & (place(slab) == p))(functools.partial(role_client, p, far))


def body(n_slab, n_det, traces, tables, slab_range, table_slot, sample_start):
    _, frames, samp = traces.shape
    voxels = tables.shape[2]
    pair, n_chunk, far_chunks = sizes(n_slab, n_det, frames)
    far_rows = max(len(far_chunks), 1) * ROWS
    head = ROWS // SUBLANES
    n_tile = samp // LANES
    tiled = traces.reshape(frames // SUBLANES, SUBLANES, n_tile, LANES).transpose(0, 2, 1, 3)
    wide = NTAB * KWIN
    anywhere = pl.BlockSpec(memory_space=pl.ANY)
    dma = pltpu.SemaphoreType.DMA
    bf16, f32 = jnp.bfloat16, jnp.float32
    return pl.pallas_call(
        functools.partial(kernel, n_slab, n_det),
        out_shape=pltpu.VMEM((frames, voxels), f32),
        in_specs=[anywhere] * 5,
        out_specs=pl.BlockSpec(memory_space=pltpu.VMEM),
        scratch_shapes=[
            pltpu.VMEM((head, n_tile, SUBLANES, LANES), f32),
            pltpu.VMEM((frames // SUBLANES, n_tile, SUBLANES, LANES), f32),
            pltpu.VMEM(tables.shape, bf16),
            pltpu.SMEM(slab_range.shape, jnp.int32),
            pltpu.SMEM(table_slot.shape, jnp.int32),
            pltpu.SMEM(sample_start.shape, jnp.int32),
            pltpu.VMEM((OFFSETS, frames, KWIN), bf16),
            pltpu.VMEM((pair, OFFSETS, frames, KWIN), bf16),
            pltpu.VMEM((pair, OFFSETS, far_rows, KWIN), bf16),
            pltpu.VMEM((OFFSETS, 1, LANES), f32),
            pltpu.VMEM((pair, OFFSETS, 1, LANES), f32),
            pltpu.VMEM((pair, OFFSETS, 1, LANES), f32),
            pltpu.VMEM((pair, frames, wide), f32),
            pltpu.VMEM((pair, frames, wide), bf16),
            pltpu.VMEM((pair, frames, wide), bf16),
            pltpu.VMEM((pair, frames, wide), bf16),
            pltpu.VMEM((pair, frames, wide), bf16),
            dma((2,)),
            dma,
            dma((3,)),
            dma,
            dma,
            dma((n_chunk, pair)),
            dma,
            dma((pair,)),
            dma,
            dma((pair,)),
            dma,
            dma((n_chunk, pair)),
            dma,
            dma,
            dma((n_chunk, pair)),
        ],
        compiler_params=pltpu.CompilerParams(
            collective_id=0, has_side_effects=True, vmem_limit_bytes=66_500_000
        ),
    )(tiled, tables, slab_range, table_slot, sample_start)


def solution(mesh):
    placed = (
        P(("slab", "det"), None, None),
        P("slab", None, "det"),
        P(("slab", "det"), None),
        P(("slab", "det"), None),
        P(("slab", "det"), None),
    )
    return jax.shard_map(
        functools.partial(body, mesh.shape["slab"], mesh.shape["det"]),
        mesh=mesh, in_specs=placed, out_specs=P(None, ("slab", "det")), check_vma=False,
    )
```

time: 19.9 us -> 19.6 us (0.985)
  Pallas kernels: 19 us -> 18.7 us
    pallas_call x1, Pallas kernels: 19 us -> 18.7 us  [body(): pl.pallas_call(functools.partial(kernel, n_slab, n_det), out_shape=pltpu....]
where the time goes in v5:
time: 19.6 us; the launch traced here: 19.4 us
  Pallas kernels  18.7 us (95%)
  local copies, waits for them, and re-layouts  0.71 us (4%)
    pallas_call x1, Pallas kernels, body(): pl.pallas_call(functools.partial(kernel, n_slab, n_det), out_shape=pltpu....  18.7 us
    unnamed x1, local copies, waits for them, and re-layouts  0.71 us

profile of v5, /device:TPU:0, one launch (start us, length us, event | category | flops | bytes accessed | tf_op | source)
XLA Modules:
  0.0 19.4 jit_solution(18055478138031323060)
XLA Ops:
  0.0 18.7 %shard_map.55 = f32[128,512]{1,0:T(8,128)S(1)} custom-call(f32[16,32,8,128]{3,2,1,0:T(8,128)} %bitcast.3, bf16[4,256,512]{2,1,0:T(8,128)(2,1)} %tables.1, s32[1,2]{1,0:T(1,128)} %slab_range.1, s32[1,7]{1,0:T(1,128)} %table_slot.1, s32[1,7]{1,0:T(1,128)} %sample_start.1), custom_call_target="tpu_custom_call" | custom-call | tf_op jit(solution)/shard_map/pallas_call | solution.py:406
  18.7 0.7 %copy.7 = f32[128,512]{1,0:T(8,128)} copy(f32[128,512]{1,0:T(8,128)S(1)} %shard_map.55) | data formatting | bytes 524288

commit v6 on v5

--- a/solution.py
+++ b/solution.py
@@ -15,7 +15,7 @@
 SUBLANES = 8
 OFFSETS = 2 * RANGE + 1
 ROWS = 16
-LAG = 5
+LAG = 6
 DIRECT = 2
 SKIP = 0
 AHEAD = 1
@@ -32,7 +32,7 @@
 def kernel(
     n_slab, n_det,
     traces, tables, slab_range, table_slot, sample_start, out,
-    first_buf, rest_buf, table_buf, range_buf, slot_buf, start_buf,
+    first_buf, next_buf, rest_buf, table_buf, range_buf, slot_buf, start_buf,
     send_win, got_win, far_win, send_mask, got_mask, far_mask,
     own, up, from_outer, from_inner, down,
     trace_sem, table_sem, small_sem,
@@ -67,7 +67,12 @@
         pltpu.make_async_copy(
             traces.at[pl.ds(at_step(0) * groups, groups)], first_buf, trace_sem.at[0]
         ),
-        pltpu.make_async_copy(traces, rest_buf, trace_sem.at[1]),
+        pltpu.make_async_copy(
+            traces.at[pl.ds(0, next_buf.shape[0])], next_buf, trace_sem.at[1]
+        ),
+        pltpu.make_async_copy(
+            traces.at[pl.ds(next_buf.shape[0], rest_buf.shape[0])], rest_buf, trace_sem.at[2]
+        ),
     ]
     for copy in loads:
         copy.start()
@@ -129,7 +134,6 @@
             heard = heard + jnp.where(there, jnp.where(is_host, pair, 1), 0)
 
     table_load = pltpu.make_async_copy(tables, table_buf, table_sem)
-    table_load.start()
 
     for p in range(pair):
         for o in range(OFFSETS):
@@ -191,7 +195,10 @@
 
     def window(k, o):
         c = at_step(k)
-        buf, base = (first_buf, 0) if k == 0 else (rest_buf, c * groups)
+        buf, base = first_buf, 0
+        if k:
+            early = max(edge_order[k], order[k]) < next_buf.shape[0] // groups
+            buf, base = (next_buf, c * groups) if early else (rest_buf, c * groups - next_buf.shape[0])
         for i in range(KWIN // LANES):
             pieces = []
             for g in range(groups):
@@ -232,8 +239,10 @@
             )
 
     for k in range(n_chunk):
-        if k < len(loads):
+        if k < 2:
             loads[k].wait()
+        if k * groups == next_buf.shape[0]:
+            loads[2].wait()
         for o in range(OFFSETS):
             window(k, o)
         if k == 0:
@@ -242,6 +251,8 @@
                 send(p)
         for p in range(pair):
             send(p, k)
+
+    table_load.start()
 
     def stack(c, p, far):
         wins, masks, sem = (
@@ -397,6 +408,7 @@
     pair, n_chunk, far_chunks = sizes(n_slab, n_det, frames)
     far_rows = max(len(far_chunks), 1) * ROWS
     head = ROWS // SUBLANES
+    soon = len(far_chunks) + AHEAD
     n_tile = samp // LANES
     tiled = traces.reshape(frames // SUBLANES, SUBLANES, n_tile, LANES).transpose(0, 2, 1, 3)
     wide = NTAB * KWIN
@@ -410,7 +422,8 @@
         out_specs=pl.BlockSpec(memory_space=pltpu.VMEM),
         scratch_shapes=[
             pltpu.VMEM((head, n_tile, SUBLANES, LANES), f32),
-            pltpu.VMEM((frames // SUBLANES, n_tile, SUBLANES, LANES), f32),
+            pltpu.VMEM((soon * head, n_tile, SUBLANES, LANES), f32),
+            pltpu.VMEM((frames // SUBLANES - soon * head, n_tile, SUBLANES, LANES), f32),
             pltpu.VMEM(tables.shape, bf16),
             pltpu.SMEM(slab_range.shape, jnp.int32),
             pltpu.SMEM(table_slot.shape, jnp.int32),
@@ -426,7 +439,7 @@
             pltpu.VMEM((pair, frames, wide), bf16),
             pltpu.VMEM((pair, frames, wide), bf16),
             pltpu.VMEM((pair, frames, wide), bf16),
-            dma((2,)),
+            dma((3,)),
             dma,
             dma((3,)),
             dma,

time: 19.6 us -> 19.3 us (0.985)
  Pallas kernels: 18.7 us -> 18.5 us
    pallas_call x1, Pallas kernels: 18.7 us -> 18.5 us  [body(): pl.pallas_call(functools.partial(kernel, n_slab, n_det), out_shape=pltpu....]
where the time goes in v6:
time: 19.3 us; the launch traced here: 19.2 us
  Pallas kernels  18.5 us (96%)
  local copies, waits for them, and re-layouts  0.71 us (4%)
    pallas_call x1, Pallas kernels, body(): pl.pallas_call(functools.partial(kernel, n_slab, n_det), out_shape=pltpu....  18.5 us
    unnamed x1, local copies, waits for them, and re-layouts  0.71 us

profile of v6, /device:TPU:0, one launch (start us, length us, event | category | flops | bytes accessed | tf_op | source)
XLA Modules:
  0.0 19.2 jit_solution(16870901162183212599)
XLA Ops:
  0.0 18.5 %shard_map.55 = f32[128,512]{1,0:T(8,128)S(1)} custom-call(f32[16,32,8,128]{3,2,1,0:T(8,128)} %bitcast.3, bf16[4,256,512]{2,1,0:T(8,128)(2,1)} %tables.1, s32[1,2]{1,0:T(1,128)} %slab_range.1, s32[1,7]{1,0:T(1,128)} %table_slot.1, s32[1,7]{1,0:T(1,128)} %sample_start.1), custom_call_target="tpu_custom_call" | custom-call | tf_op jit(solution)/shard_map/pallas_call | solution.py:418
  18.5 0.7 %copy.7 = f32[128,512]{1,0:T(8,128)} copy(f32[128,512]{1,0:T(8,128)S(1)} %shard_map.55) | data formatting | bytes 524288

commit v7 on v6

--- a/solution.py
+++ b/solution.py
@@ -19,7 +19,8 @@
 DIRECT = 2
 SKIP = 0
 AHEAD = 1
-DOT = 32
+TAIL = 2
+DOT = 16
 
 
 def sizes(n_slab, n_det, frames):
@@ -361,7 +362,8 @@
             if p < pair - 1:
                 client_copy(c, p).start()
 
-        tasks = [(c, p) for c in order for p in range(pair)]
+        tasks = [(c, p) for c in order[:-TAIL] for p in range(pair)]
+        tasks += [(c, p) for p in range(pair) for c in order[-TAIL:]]
         if cross:
             for i in range(len(tasks) + LAG):
                 if i < len(tasks):

time: 19.3 us -> 19 us (0.984)
  Pallas kernels: 18.5 us -> 18.1 us
    pallas_call x1, Pallas kernels: 18.5 us -> 18.1 us  [body(): pl.pallas_call(functools.partial(kernel, n_slab, n_det), out_shape=pltpu....]
where the time goes in v7:
time: 19 us; the launch traced here: 18.8 us
  Pallas kernels  18.1 us (95%)
  local copies, waits for them, and re-layouts  0.71 us (4%)
    pallas_call x1, Pallas kernels, body(): pl.pallas_call(functools.partial(kernel, n_slab, n_det), out_shape=pltpu....  18.1 us
    unnamed x1, local copies, waits for them, and re-layouts  0.71 us

profile of v7, /device:TPU:0, one launch (start us, length us, event | category | flops | bytes accessed | tf_op | source)
XLA Modules:
  0.0 18.8 jit_solution(12998693595574748436)
XLA Ops:
  0.0 18.1 %shard_map.55 = f32[128,512]{1,0:T(8,128)S(1)} custom-call(f32[16,32,8,128]{3,2,1,0:T(8,128)} %bitcast.3, bf16[4,256,512]{2,1,0:T(8,128)(2,1)} %tables.1, s32[1,2]{1,0:T(1,128)} %slab_range.1, s32[1,7]{1,0:T(1,128)} %table_slot.1, s32[1,7]{1,0:T(1,128)} %sample_start.1), custom_call_target="tpu_custom_call" | custom-call | tf_op jit(solution)/shard_map/pallas_call | solution.py:420
  18.1 0.7 %copy.7 = f32[128,512]{1,0:T(8,128)} copy(f32[128,512]{1,0:T(8,128)S(1)} %shard_map.55) | data formatting | bytes 524288
